TPU v7x, 128 devices: a whole 4x4x4 slice. The times are simulated.
128 devices in a mesh: asset: 32 (over y, z, core), tm: 4 (over x).
Axes of the slice: x: 4, y: 4, z: 4, core: 2. Of those that a mesh axis runs over, the one named last changes fastest.
Arguments:
- values: float32 [4, 1024, 65536], P(None, 'tm', 'asset'), may hold values from -64 to 64
- listed_from: int32 [65536], P('asset'), may hold values from -1024 to 1023, as said below
- listed_until: int32 [65536], P('asset'), may hold values from -960 to 3070, as said below
Outputs:
- standardized: float32 [4, 1024, 65536], P(None, 'tm', 'asset')
Inputs may be any that keep to these rules, and one draw needn't show every extreme that they name: listed_until[a] - listed_from[a] is at least 64. listed_until[a] - listed_from[a] is at least 64.
All inputs are finite; a program needn't handle non-finite values.
Results may differ from a plain program's by a relative error of at most 0.00005.
Values sent between devices are 32-bit elements; how exact they have to be, the bound alone decides.
A program may use at most 128 MiB of HBM per device.

v0:
```python
import jax
import jax.numpy as jnp
from jax import lax
from jax.sharding import PartitionSpec as P

WINDOW = 64


def passed_along(block, axis, distance):
    devices = range(lax.axis_size(axis))
    route = [(i - distance, i) for i in devices if i - distance in devices]
    return lax.ppermute(block, axis, route)


def sent_to_all(x, axis):
    copies = jnp.broadcast_to(x, (lax.axis_size(axis), *x.shape))
    return lax.all_to_all(copies, axis, split_axis=0, concat_axis=0, tiled=True)


def of_everyone(x, axis):
    everything = sent_to_all(x, axis)
    return jnp.sum(everything, axis=0)


def in_one(arrays, axis):
    line, at, finished = (jnp.concatenate([a.reshape(-1) for a in arrays]), 0, [])
    running = of_everyone(line, axis)
    for a in arrays:
        finished.append(running[at : at + a.size].reshape(a.shape))
        at += a.size
    return tuple(finished)


def listing(stamps, listed_from, listed_until):
    opened = listed_from[None, :]
    closed = listed_until[None, :]
    weight = ((stamps >= opened) & (stamps < closed)).astype(jnp.float32)
    window_low = jnp.maximum(jnp.maximum(stamps - (WINDOW - 1), opened), 0)
    window_high = jnp.minimum(stamps, closed - 1)
    counted = jnp.maximum(window_high - window_low + 1, 1)
    return (weight, counted.astype(jnp.float32))


def window_sums(masked):
    field_count, row_count, asset_count = masked.shape
    blocks = row_count // WINDOW
    current = masked.reshape(field_count, blocks, WINDOW, asset_count)
    offset = jnp.arange(WINDOW, dtype=jnp.int32)
    lower_band = (offset[None, :] <= offset[:, None]).astype(jnp.float32)
    upper_band = (offset[None, :] > offset[:, None]).astype(jnp.float32)
    highest = lax.Precision.HIGHEST
    within = jnp.einsum("ij,fbja->fbia", lower_band, current, precision=highest)
    tail_rows = passed_along(masked[:, row_count - WINDOW :], "tm", 1)
    carried = jnp.einsum("ij,fja->fia", upper_band, tail_rows, precision=highest)
    earlier = jnp.einsum("ij,fbja->fbia", upper_band, current[:, : blocks - 1], precision=highest)
    spread_in = jnp.concatenate([carried[:, None], earlier], axis=1)
    return (within + spread_in).reshape(field_count, row_count, asset_count)


def standardize(field_values, weight, count_part, count_total):
    local_sum = jnp.sum(field_values * weight[None], axis=2)
    local_sq = jnp.sum(weight[None] * field_values * field_values, axis=2)
    if count_total is None:
        count_total, totals, squares = in_one((count_part, local_sum, local_sq), "asset")
    else:
        totals, squares = in_one((local_sum, local_sq), "asset")
    count_floor = jnp.maximum(count_total, 1.0)[None, :]
    center = totals / count_floor
    spread = jnp.maximum(squares / count_floor - center * center, 0.0)
    deviate = (field_values - center[:, :, None]) * weight[None]
    return (deviate / jnp.sqrt(spread + 0.1)[:, :, None], count_total)


def per_device(values, listed_from, listed_until):
    field_count, row_count, asset_count = values.shape
    stamps = lax.axis_index("tm") * row_count + lax.broadcasted_iota(
        jnp.int32, (row_count, asset_count), 0
    )
    weight, counted = listing(stamps, listed_from, listed_until)
    masked = values * weight[None]
    rolling = window_sums(masked) / counted[None]
    count_part = jnp.sum(weight, axis=1)
    scored, count_total = standardize(rolling, weight, count_part, None)
    clipped = jnp.clip(scored, -3.0, 3.0)
    result_field, unused = standardize(clipped, weight, None, count_total)
    return result_field


def solution(mesh):
    in_specs = (P(None, "tm", "asset"), P("asset"), P("asset"))
    out_specs = P(None, "tm", "asset")
    return jax.shard_map(
        per_device, mesh=mesh, in_specs=in_specs, out_specs=out_specs, check_vma=False
    )
```

profile of v0, /device:TPU:1, one launch (start us, length us, event | category | flops | bytes accessed | tf_op | source)
XLA Modules:
  0.0 117.4 jit_solution(9558186845676015570)
XLA Ops:
  0.0 1.1 and_convert_fusion.1
  1.1 0.0 copy-start.1
  1.1 0.0 copy-start.2
  1.1 0.0 copy-start.3
  1.1 5.4 %broadcast_multiply_fusion = f32[4,256,2048]{2,1,0:T(8,128)S(1)} fusion(f32[4,256,2048]{2,1,0:T(8,128)} %param.3, f32[256,2048]{1,0:T(8,128)S(1)} %and_convert_fusion.1), kind=kLoop, calls=%fused_computation.17 | loop fusion | flops 2097152 | bytes 18874368 | tf_op jit(solution)/shard_map/mul | solution.py:80
  6.6 0.0 copy-done.1
  6.6 0.2 slice.72
  6.8 4.1 %collective-permute-start = (f32[4,64,2048]{2,1,0:T(8,128)S(1)}, f32[4,64,2048]{2,1,0:T(8,128)S(1)}, u32[]{:S(2)}, u32[]{:S(2)}) collective-permute-start(f32[4,64,2048]{2,1,0:T(8,128)S(1)} %slice.72), channel_id=1, source_target_pairs={{0,1},{1,2},{2,3},{4,5},{5,6},{6,7},{8,9},{9,10},{10,11},{12,13},{... | collective-permute-start | bytes 6291464 | tf_op jit(solution)/shard_map/ppermute | solution.py:12
  10.9 0.0 copy-done.2
  10.9 0.0 copy-done.3
  10.9 0.5 fusion.9
  11.4 0.4 and_convert_fusion
  11.8 0.8 maximum_convert_fusion
  12.6 0.0 copy-start
  12.6 6.3 %convolution_bitcast_fusion = f32[4,3,64,2048]{3,2,1,0:T(8,128)} fusion(f32[4,4,64,2048]{3,2,1,0:T(8,128)S(1)} %bitcast.43), kind=kOutput, calls=%fused_computation.18 | convolution fusion | flops 1207963648 | bytes 14680064 | tf_op jit(solution)/shard_map/ij,fbja->fbia/dot_general | solution.py:55
  18.9 36.1 %collective-permute-done = f32[4,64,2048]{2,1,0:T(8,128)S(1)} collective-permute-done((f32[4,64,2048]{2,1,0:T(8,128)S(1)}, f32[4,64,2048]{2,1,0:T(8,128)S(1)}, u32[]{:S(2)}, u32[]{:S(2)}) %collective-permute-start) | collective-permute-done | bytes 2097184 | tf_op jit(solution)/shard_map/ppermute | solution.py:12
  55.0 1.4 %convolution_bitcast_fusion.1 = f32[4,1,64,2048]{3,2,1,0:T(8,128)S(1)} fusion(f32[4,64,2048]{2,1,0:T(8,128)S(1)} %collective-permute-done), kind=kOutput, calls=%fused_computation.19 | convolution fusion | flops 402657280 | bytes 4194304 | tf_op jit(solution)/shard_map/ij,fja->fia/dot_general | solution.py:54
  56.4 0.0 copy-done
  56.4 12.8 %multiply_reduce_fusion.1 = (f32[4,4,64]{2,1,0:T(4,128)S(1)}, f32[4,4,64]{2,1,0:T(4,128)S(1)}, f32[4,4,64,2048]{3,2,1,0:T(8,128)}) fusion(f32[4,64,2048]{2,1,0:T(8,128)S(1)} %and_convert_fusion, f32[4,64,2048]{2,1,0:T(8,128)S(1)} %maximum_convert_fusion, f32[4,3,64,2048]{3,2,1,0:T(8,128)} %convolution_bitcast_fusion, ...), kind=kOutput, calls=%fused_computation.3 | convolution fusion | flops 1625294848 | bytes 29368320 | tf_op jit(solution)/shard_map/ij,fbja->fbia/dot_general | solution.py:52
  69.2 0.1 reshape.233
  69.2 0.1 reshape.234
  69.3 0.9 broadcast_in_dim.7
  70.2 9.6 %all-to-all-start = ((f32[32,1,2304]{2,1,0:T(1,128)}), f32[32,1,2304]{2,1,0:T(1,128)S(1)}, u32[]{:S(2)}, u32[]{:S(2)}) async-start(f32[32,1,2304]{2,1,0:T(1,128)} %broadcast_in_dim.7), calls=%async_computation | async-start | bytes 589824 | tf_op jit(solution)/shard_map/all_to_all | solution.py:17
  79.8 9.3 %all-to-all-done = f32[32,1,2304]{2,1,0:T(1,128)S(1)} async-done(((f32[32,1,2304]{2,1,0:T(1,128)}), f32[32,1,2304]{2,1,0:T(1,128)S(1)}, u32[]{:S(2)}, u32[]{:S(2)}) %all-to-all-start) | async-done | bytes 294944 | tf_op jit(solution)/shard_map/all_to_all | solution.py:17
  89.1 0.2 reduce_sum.66
  89.4 0.1 div.75
  89.4 0.1 sub.59
  89.5 6.6 %multiply_reduce_fusion = (f32[4,4,64]{2,1,0:T(4,128)S(1)}, f32[4,4,64]{2,1,0:T(4,128)S(1)}) fusion(f32[4,64,2048]{2,1,0:T(8,128)S(1)} %and_convert_fusion, f32[4,4,64]{2,1,0:T(4,128)S(1)} %div.75, f32[4,4,64]{2,1,0:T(4,128)S(1)} %sub.59, f32[4,4,64,2048]{3,2,1,0:T(8,128)} %get-tuple-element.17, f32[4,64,2048]{2,1,0:T(8,128)} %copy-done), kind=kLoop, calls=%fused_computation.1 | loop fusion | flops 18872320 | bytes 12599296 | tf_op jit(solution)/shard_map/reduce_sum | solution.py:61
  96.1 0.1 reshape.235
  96.2 0.1 reshape.236
  96.2 0.8 broadcast_in_dim.8
  97.1 3.7 %all-to-all-start.1 = ((f32[32,1,2048]{2,1,0:T(1,128)}), f32[32,1,2048]{2,1,0:T(1,128)S(1)}, u32[]{:S(2)}, u32[]{:S(2)}) async-start(f32[32,1,2048]{2,1,0:T(1,128)} %broadcast_in_dim.8), calls=%async_computation.1 | async-start | bytes 524288 | tf_op jit(solution)/shard_map/all_to_all | solution.py:17
  100.8 0.8 maximum_convert_fusion.1
  101.6 8.2 %all-to-all-done.1 = f32[32,1,2048]{2,1,0:T(1,128)S(1)} async-done(((f32[32,1,2048]{2,1,0:T(1,128)}), f32[32,1,2048]{2,1,0:T(1,128)S(1)}, u32[]{:S(2)}, u32[]{:S(2)}) %all-to-all-start.1) | async-done | bytes 262176 | tf_op jit(solution)/shard_map/all_to_all | solution.py:17
  109.8 0.2 reduce_sum.69
  110.1 7.3 %fusion.8 = f32[4,256,2048]{2,1,0:T(8,128)} fusion(f32[4,4,64,2048]{3,2,1,0:T(8,128)} %get-tuple-element.17, f32[4,256]{1,0:T(4,128)S(1)} %get-tuple-element.14, f32[4,256]{1,0:T(4,128)S(1)} %get-tuple-element.13, f32[4,256]{1,0:T(4,128)S(1)} %get-tuple-element.16, f32[4,256]{1,0:T(4,128)S(1)} %get-tuple-element.15, ...), kind=kLoop, calls=%fused_computation.14 | loop fusion | flops 16777216 | bytes 20987904 | tf_op jit(solution)/shard_map/div | solution.py:71
  (15 shorter events, 0.1 us)
Async XLA Ops:
  1.1 5.5 %copy-start.1 = (f32[256,2048]{1,0:T(8,128)}, f32[256,2048]{1,0:T(8,128)S(1)}, u32[]{:S(2)}) copy-start(f32[256,2048]{1,0:T(8,128)S(1)} %and_convert_fusion.1) | copy-start | bytes 6291460
  1.1 9.8 %copy-start.2 = (s32[2048]{0:T(1024)S(1)}, s32[2048]{0:T(1024)}, u32[]{:S(2)}) copy-start(s32[2048]{0:T(1024)} %param.4) | copy-start | bytes 24580
  1.1 9.8 %copy-start.3 = (s32[2048]{0:T(1024)S(1)}, s32[2048]{0:T(1024)}, u32[]{:S(2)}) copy-start(s32[2048]{0:T(1024)} %param.5) | copy-start | bytes 24580
  6.8 48.2 %collective-permute-start = (f32[4,64,2048]{2,1,0:T(8,128)S(1)}, f32[4,64,2048]{2,1,0:T(8,128)S(1)}, u32[]{:S(2)}, u32[]{:S(2)}) collective-permute-start(f32[4,64,2048]{2,1,0:T(8,128)S(1)} %slice.72), channel_id=1, source_target_pairs={{0,1},{1,2},{2,3},{4,5},{5,6},{6,7},{8,9},{9,10},{10,11},{12,13},{... | collective-permute-start | bytes 6291464 | tf_op jit(solution)/shard_map/ppermute | solution.py:12
  12.6 43.8 %copy-start = (f32[4,64,2048]{2,1,0:T(8,128)}, f32[4,64,2048]{2,1,0:T(8,128)S(1)}, u32[]{:S(2)}) copy-start(f32[4,64,2048]{2,1,0:T(8,128)S(1)} %maximum_convert_fusion) | copy-start | bytes 6291460
  70.2 18.9 %all-to-all-start = ((f32[32,1,2304]{2,1,0:T(1,128)}), f32[32,1,2304]{2,1,0:T(1,128)S(1)}, u32[]{:S(2)}, u32[]{:S(2)}) async-start(f32[32,1,2304]{2,1,0:T(1,128)} %broadcast_in_dim.7), calls=%async_computation | async-start | bytes 589824 | tf_op jit(solution)/shard_map/all_to_all | solution.py:17
  97.1 12.8 %all-to-all-start.1 = ((f32[32,1,2048]{2,1,0:T(1,128)}), f32[32,1,2048]{2,1,0:T(1,128)S(1)}, u32[]{:S(2)}, u32[]{:S(2)}) async-start(f32[32,1,2048]{2,1,0:T(1,128)} %broadcast_in_dim.8), calls=%async_computation.1 | async-start | bytes 524288 | tf_op jit(solution)/shard_map/all_to_all | solution.py:17
where the time goes:
time: 118 us; the launch traced here: 117 us
  waiting for transfers between devices  53.6 us (45%)
  other arithmetic  23.3 us (20%)
  matrix products  20.4 us (17%)
  starting transfers between devices  17.4 us (15%)
  local copies, waits for them, and re-layouts  2.47 us (2%)
    ppermute x1, waiting for transfers between devices, passed_along(): return lax.ppermute(block, axis, route)  36.1 us
    all_to_all x2, waiting for transfers between devices, sent_to_all(): return lax.all_to_all(copies, axis, split_axis=0, concat_axis=0, tiled=True)  17.5 us
    all_to_all x2, starting transfers between devices, sent_to_all(): return lax.all_to_all(copies, axis, split_axis=0, concat_axis=0, tiled=True)  13.3 us
    dot_general x1, matrix products, window_sums(): within = jnp.einsum('ij,fbja->fbia', lower_band, current, precision=highest)  12.8 us
    div x1, other arithmetic, standardize(): return (deviate / jnp.sqrt(spread + 0.1)[:, :, None], count_total)  7.32 us
    reduce_sum x1, other arithmetic, standardize(): local_sum = jnp.sum(field_values * weight[None], axis=2)  6.55 us
    dot_general x1, matrix products, window_sums(): jnp.einsum('ij,fbja->fbia', upper_band, current[:, :blocks - 1], precisio...  6.31 us
    mul x1, other arithmetic, per_device(): masked = values * weight[None]  5.44 us
  transfers between devices with their start and end apart: 3, of which 3 were waited for; matrix products, arithmetic and copies ran while one was open for 8% of the time, Pallas kernels for 0%

commit v1 on v0

v1 whole, which is shorter than its diff:
```python
import functools

import jax
import jax.numpy as jnp
from jax import lax
from jax.experimental import pallas as pl
from jax.experimental.pallas import tpu as pltpu
from jax.sharding import PartitionSpec as P

WINDOW = 64
TILE = 8
LANES = 128
CHUNK = 512
MESH = pl.DeviceIdType.MESH


def kernel(
    sizes,
    vals,
    opened,
    closed,
    out,
    halo,
    hop1,
    hop2,
    ring,
    total,
    base,
    ahead,
    pivot,
    msg_b1,
    msg_b2,
    msg_h1,
    msg_h2,
    got_b1,
    got_b2,
    got_h1,
    got_h2,
    count_b,
    count_h,
    floor_b,
    floor_h,
    row_b1,
    row_b2,
    row_h1,
    row_h2,
    load_sem,
    direct_send,
    back_send,
    relay1_send,
    relay2_send,
    halo_recv,
    hop1_recv,
    hop2_recv,
    ex_send,
    ex_recv,
):
    blocks_t, peers = sizes
    fields, rows, assets = vals.shape
    tiles = rows // TILE
    wt = WINDOW // TILE
    chunks = assets // CHUNK
    bulk = tiles - wt
    back_field = fields - 1
    x = lax.axis_index("tm")
    me = lax.axis_index("asset")
    nxt = lax.rem(x + 1, blocks_t)
    prv = lax.rem(x + blocks_t - 1, blocks_t)
    t0 = x * rows

    def load(f, b):
        part = pl.ds(b * WINDOW, WINDOW)
        return pltpu.make_async_copy(
            vals.at[f, part, :], out.at[f, part, :], load_sem.at[f, b]
        )

    for b in range(rows // WINDOW):
        for f in range(fields):
            load(f, b).start()

    barrier = pltpu.get_barrier_semaphore()
    for t in (nxt, prv):
        pl.semaphore_signal(barrier, 1, device_id={"tm": t}, device_id_type=MESH)

    def greet(k, carry):
        peer = lax.rem(me + k, peers)
        pl.semaphore_signal(barrier, 1, device_id={"asset": peer}, device_id_type=MESH)
        return carry

    lax.fori_loop(1, peers, greet, 0)
    pl.semaphore_wait(barrier, peers + 1)

    tail = rows - WINDOW

    def tile_rows(r):
        return pl.ds(r * TILE, TILE)

    def direct(f, r):
        return pltpu.make_async_remote_copy(
            src_ref=vals.at[f, pl.ds(tail + r * TILE, TILE), :],
            dst_ref=halo.at[f, tile_rows(r), :],
            send_sem=direct_send,
            recv_sem=halo_recv.at[f, r],
            device_id={"tm": nxt},
            device_id_type=MESH,
        )

    def back(r):
        return pltpu.make_async_remote_copy(
            src_ref=vals.at[back_field, pl.ds(tail + r * TILE, TILE), :],
            dst_ref=hop1.at[tile_rows(r), :],
            send_sem=back_send,
            recv_sem=hop1_recv.at[r],
            device_id={"tm": prv},
            device_id_type=MESH,
        )

    def relay1(r):
        return pltpu.make_async_remote_copy(
            src_ref=hop1.at[tile_rows(r), :],
            dst_ref=hop2.at[tile_rows(r), :],
            send_sem=relay1_send,
            recv_sem=hop2_recv.at[r],
            device_id={"tm": prv},
            device_id_type=MESH,
        )

    def relay2(r):
        return pltpu.make_async_remote_copy(
            src_ref=hop2.at[tile_rows(r), :],
            dst_ref=halo.at[back_field, tile_rows(r), :],
            send_sem=relay2_send,
            recv_sem=halo_recv.at[back_field, r],
            device_id={"tm": prv},
            device_id_type=MESH,
        )

    has_next = x < blocks_t - 1
    order = list(range(wt - 1, -1, -1))

    @pl.when(has_next)
    def _():
        for r in order:
            back(r).start()
            for f in range(back_field):
                direct(f, r).start()

    def exchange(g, msg, got, k):
        return pltpu.make_async_remote_copy(
            src_ref=msg,
            dst_ref=got.at[k],
            send_sem=ex_send.at[g],
            recv_sem=ex_recv.at[g],
            device_id={"asset": lax.rem(me + k, peers)},
            device_id_type=MESH,
        )

    def exchange_start(g, msg, got):
        def one(k, carry):
            exchange(g, msg, got, k).start()
            return carry

        lax.fori_loop(1, peers, one, 0)
        got[0] = msg[...]

    def exchange_all(g, got):
        others = got.at[pl.ds(1, peers - 1)]
        return pltpu.make_async_remote_copy(
            src_ref=others,
            dst_ref=others,
            send_sem=ex_send.at[g],
            recv_sem=ex_recv.at[g],
            device_id={"asset": me},
            device_id_type=MESH,
        )

    sub = lax.broadcasted_iota(jnp.int32, (TILE, LANES), 0)
    lane = lax.broadcasted_iota(jnp.int32, (TILE, LANES), 1)
    subc = lax.broadcasted_iota(jnp.int32, (TILE, CHUNK), 0)
    width = fields * TILE

    def lanes(c):
        return pl.ds(c * CHUNK, CHUNK)

    def fold(v):
        acc = v[:, :LANES]
        for i in range(1, CHUNK // LANES):
            acc = acc + v[:, i * LANES : (i + 1) * LANES]
        return acc

    def across(v):
        return jnp.sum(v, axis=1, keepdims=True)

    def flat(columns):
        z = jnp.zeros((TILE, LANES), jnp.float32)
        for at, column in columns:
            z = jnp.where(lane == sub + at, column, z)
        return jnp.sum(z, axis=0, keepdims=True)

    def column(row, at):
        return across(jnp.where(lane == sub + at, row, 0.0))

    def listed(c, first):
        t = subc + first
        o = opened[:, lanes(c)]
        u = closed[:, lanes(c)]
        return t, o, u, (t >= o) & (t < u)

    def share(t, o, u, w):
        low = jnp.maximum(jnp.maximum(t - (WINDOW - 1), o), 0)
        high = jnp.minimum(t, u - 1)
        counted = jnp.maximum(high - low + 1, 1).astype(jnp.float32)
        return jnp.where(w, 1.0 / counted, 0.0)

    def moments(n, s, q, pivots):
        count = across(n)
        inverse = 1.0 / jnp.maximum(count, 1.0)
        columns = []
        means = []
        for f in range(fields):
            s_f, q_f = across(s[f]), across(q[f])
            lift = s_f * inverse
            mean = pivots[f] + lift
            means.append(mean)
            columns.append((f * TILE, mean))
            columns.append((width + f * TILE, jnp.maximum(q_f - s_f * lift, 0.0)))
        return count, means, columns

    def counts_at(count, at):
        return [(at + f * TILE, count) for f in range(fields)]

    zero = jnp.zeros((TILE, LANES), jnp.float32)

    msg_b1[...] = jnp.zeros_like(msg_b1)
    base[...] = jnp.zeros_like(base)
    for f in range(fields):
        load(f, 0).wait()

    def prefix(f, c, w, v):
        p = jnp.where(w, v, 0.0)
        for k in (1, 2, 4):
            p = p + jnp.where(subc >= k, pltpu.roll(p, k, 0), 0.0)
        p = p + base[f, :, lanes(c)]
        base[f, :, lanes(c)] = jnp.broadcast_to(p[TILE - 1 :, :], p.shape)
        return p

    def first_tile(r, carry):
        n = zero
        here = pl.ds(pl.multiple_of(r * TILE, TILE), TILE)
        for c in range(chunks):
            _, _, _, w = listed(c, t0 + r * TILE)
            n = n + fold(jnp.where(w, 1.0, 0.0))
            for f in range(fields):
                p = prefix(f, c, w, out[f, here, lanes(c)])
                ring[f, here, lanes(c)] = p
                out[f, here, lanes(c)] = p
        msg_b1[pl.ds(r, 1), :] = flat(counts_at(across(n), 3 * width))
        return carry

    lax.fori_loop(0, wt, first_tile, 0)

    for f in range(fields):
        rough = zero
        for c in range(chunks):
            rough = rough + fold(base[f, :, lanes(c)])
        pivot[f] = jnp.broadcast_to(across(rough) * (1.0 / (WINDOW * assets)), zero.shape)

    def bulk_block(b, carry):
        total[...] = base[...]
        base[...] = jnp.zeros_like(base)

        def bulk_tile(i, carry):
            r = b * wt + i
            here = pl.ds(pl.multiple_of(r * TILE, TILE), TILE)
            slot = pl.ds(pl.multiple_of(i * TILE, TILE), TILE)
            n = zero
            s = [zero] * fields
            q = [zero] * fields
            pivots = [pivot[f][:, :1] for f in range(fields)]
            for c in range(chunks):
                t, o, u, w = listed(c, t0 + r * TILE)
                n = n + fold(jnp.where(w, 1.0, 0.0))
                part = share(t, o, u, w)
                for f in range(fields):
                    p = prefix(f, c, w, out[f, here, lanes(c)])
                    old = ring[f, slot, lanes(c)]
                    ring[f, slot, lanes(c)] = p
                    rolled = (p + (total[f, :, lanes(c)] - old)) * part
                    out[f, here, lanes(c)] = rolled
                    d = jnp.where(w, rolled - pivots[f], 0.0)
                    s[f] = s[f] + fold(d)
                    q[f] = q[f] + fold(d * d)
            count, means, columns = moments(n, s, q, pivots)
            for f in range(fields):
                pivot[f] = jnp.broadcast_to(means[f], zero.shape)
            at = pl.ds(r - wt, 1)
            msg_b1[at, :] = msg_b1[at, :] + flat(columns + counts_at(count, 2 * width))

            @pl.when(r == wt)
            def _():
                for f in range(fields):
                    ahead[f] = jnp.broadcast_to(means[f], zero.shape)

            return carry

        lax.fori_loop(0, wt, bulk_tile, 0)
        return carry

    for b in range(1, rows // WINDOW):
        for f in range(fields):
            load(f, b).wait()
    lax.fori_loop(1, rows // WINDOW, bulk_block, 0)
    exchange_start(0, msg_b1, got_b1)

    @pl.when(x != blocks_t - 2)
    def _():
        for r in order:
            back(r).wait_recv()
            relay1(r).start()

    def scaled(center, spread):
        inv = 1.0 / jnp.sqrt(jnp.maximum(spread, 0.0) + 0.1)
        wide = lax.broadcasted_iota(jnp.int32, center.shape, 1)
        return jnp.where(wide < width, center, pltpu.roll(inv, width, 1))

    def merge(got, counts, floor, m2, rows_out):
        shape = rows_out.shape

        def add(p, acc):
            return acc + counts[p] * got[p]

        center = lax.fori_loop(0, peers, add, jnp.zeros(shape, jnp.float32)) / floor[...]

        def add2(p, acc):
            d = got[p] - center
            return acc + counts[p] * d * d

        between = lax.fori_loop(0, peers, add2, jnp.zeros(shape, jnp.float32))
        rows_out[...] = scaled(center, (between + m2) / floor[...])

    def summed(got, shape):
        return lax.fori_loop(
            0, peers, lambda p, acc: acc + got[p], jnp.zeros(shape, jnp.float32)
        )

    def left(v, by):
        return pltpu.roll(v, LANES - by, 1)

    def clip_tile(r, row, row_in, msg, msg_row):
        here = pl.ds(pl.multiple_of(r * TILE, TILE), TILE)
        line = jnp.broadcast_to(row_in[pl.ds(row, 1), :], zero.shape)
        center = [column(line, f * TILE) for f in range(fields)]
        inv = [column(line, width + f * TILE) for f in range(fields)]
        s = [zero] * fields
        q = [zero] * fields
        for c in range(chunks):
            _, _, _, w = listed(c, t0 + r * TILE)
            for f in range(fields):
                y = (out[f, here, lanes(c)] - center[f]) * inv[f]
                y = jnp.where(w, jnp.clip(y, -3.0, 3.0), 0.0)
                out[f, here, lanes(c)] = y
                s[f] = s[f] + fold(y)
                q[f] = q[f] + fold(y * y)
        columns = []
        for f in range(fields):
            columns.append((f * TILE, across(s[f])))
            columns.append((width + f * TILE, across(q[f])))
        msg[pl.ds(msg_row, 1), :] = flat(columns)

    def merge2(got, floor, rows_out):
        sums = summed(got, rows_out.shape)
        center = sums / floor[...]
        spread = left(sums, width) / floor[...] - center * center
        rows_out[...] = scaled(center, spread)

    def final_tile(r, row, row_in):
        here = pl.ds(pl.multiple_of(r * TILE, TILE), TILE)
        line = jnp.broadcast_to(row_in[pl.ds(row, 1), :], zero.shape)
        center = [column(line, f * TILE) for f in range(fields)]
        inv = [column(line, width + f * TILE) for f in range(fields)]
        for c in range(chunks):
            _, _, _, w = listed(c, t0 + r * TILE)
            for f in range(fields):
                y = (out[f, here, lanes(c)] - center[f]) * inv[f]
                out[f, here, lanes(c)] = jnp.where(w, y, 0.0)

    def over(n, step):
        def one(i, carry):
            step(i)
            return carry

        lax.fori_loop(0, n, one, 0)

    exchange_all(0, got_b1).wait_recv()

    def split(p):
        v = got_b1[p]
        count_b[p] = left(v, 2 * width)
        count_h[p] = left(v[:wt, :], 3 * width)

    over(peers, split)
    sums = summed(got_b1, (bulk, LANES))
    floor_b[...] = jnp.maximum(left(sums, 2 * width), 1.0)
    floor_h[...] = jnp.maximum(left(sums[:wt, :], 3 * width), 1.0)
    merge(got_b1, count_b, floor_b, left(sums, width), row_b1)
    over(bulk, lambda i: clip_tile(i + wt, i, row_b1, msg_b2, i))
    exchange_start(1, msg_b2, got_b2)

    @pl.when(x != blocks_t - 3)
    def _():
        for r in order:
            relay1(r).wait_recv()
            relay2(r).start()

    exchange_all(1, got_b2).wait_recv()
    merge2(got_b2, floor_b, row_b2)
    over(bulk, lambda i: final_tile(i + wt, i, row_b2))

    base[...] = jnp.zeros_like(base)
    pivot[...] = ahead[...]

    def halo_tile(k):
        r = wt - 1 - k
        here = pl.ds(pl.multiple_of(r * TILE, TILE), TILE)

        @pl.when(x > 0)
        def _():
            for f in range(back_field):
                direct(f, r).wait_recv()
            relay2(r).wait_recv()

        n = zero
        s = [zero] * fields
        q = [zero] * fields
        pivots = [pivot[f][:, :1] for f in range(fields)]
        for c in range(chunks):
            t, o, u, w = listed(c, t0 + r * TILE)
            _, _, _, past = listed(c, t0 + r * TILE - WINDOW)
            past = past & (t >= WINDOW)
            n = n + fold(jnp.where(w, 1.0, 0.0))
            part = share(t, o, u, w)
            for f in range(fields):
                h = jnp.where(past, halo[f, here, lanes(c)], 0.0)
                for j in (1, 2, 4):
                    up = pltpu.roll(h, TILE - j, 0)
                    h = h + jnp.where(subc < TILE - j, up, 0.0)
                before = base[f, :, lanes(c)]
                after = jnp.where(subc < TILE - 1, pltpu.roll(h, TILE - 1, 0), 0.0)
                base[f, :, lanes(c)] = before + jnp.broadcast_to(h[:1, :], h.shape)
                rolled = (out[f, here, lanes(c)] + (before + after)) * part
                out[f, here, lanes(c)] = rolled
                d = jnp.where(w, rolled - pivots[f], 0.0)
                s[f] = s[f] + fold(d)
                q[f] = q[f] + fold(d * d)
        _, means, columns = moments(n, s, q, pivots)
        for f in range(fields):
            pivot[f] = jnp.broadcast_to(means[f], zero.shape)
        msg_h1[pl.ds(r, 1), :] = flat(columns)

    over(wt, halo_tile)
    exchange_start(2, msg_h1, got_h1)
    exchange_all(2, got_h1).wait_recv()
    m2 = left(summed(got_h1, (wt, LANES)), width)
    merge(got_h1, count_h, floor_h, m2, row_h1)
    over(wt, lambda i: clip_tile(i, i, row_h1, msg_h2, i))
    exchange_start(3, msg_h2, got_h2)
    exchange_all(3, got_h2).wait_recv()
    merge2(got_h2, floor_h, row_h2)
    over(wt, lambda i: final_tile(i, i, row_h2))

    for g, got in enumerate((got_b1, got_b2, got_h1, got_h2)):
        exchange_all(g, got).wait_send()

    @pl.when(has_next)
    def _():
        for r in order:
            back(r).wait_send()
            for f in range(back_field):
                direct(f, r).wait_send()

    @pl.when(x != blocks_t - 2)
    def _():
        for r in order:
            relay1(r).wait_send()

    @pl.when(x != blocks_t - 3)
    def _():
        for r in order:
            relay2(r).wait_send()


def per_device(blocks_t, peers, values, listed_from, listed_until):
    fields, rows, assets = values.shape
    tiles = rows // TILE
    wt = WINDOW // TILE
    bulk = tiles - wt
    f32 = jnp.float32
    vmem = pltpu.VMEM
    dma = pltpu.SemaphoreType.DMA
    scratch = [
        vmem((fields, WINDOW, assets), f32),
        vmem((WINDOW, assets), f32),
        vmem((WINDOW, assets), f32),
        vmem((fields, WINDOW, assets), f32),
        vmem((fields, TILE, assets), f32),
        vmem((fields, TILE, assets), f32),
        vmem((fields, TILE, LANES), f32),
        vmem((fields, TILE, LANES), f32),
        vmem((bulk, LANES), f32),
        vmem((bulk, LANES), f32),
        vmem((wt, LANES), f32),
        vmem((wt, LANES), f32),
        vmem((peers, bulk, LANES), f32),
        vmem((peers, bulk, LANES), f32),
        vmem((peers, wt, LANES), f32),
        vmem((peers, wt, LANES), f32),
        vmem((peers, bulk, LANES), f32),
        vmem((peers, wt, LANES), f32),
        vmem((bulk, LANES), f32),
        vmem((wt, LANES), f32),
        vmem((bulk, LANES), f32),
        vmem((bulk, LANES), f32),
        vmem((wt, LANES), f32),
        vmem((wt, LANES), f32),
        dma((fields, rows // WINDOW)),
        dma,
        dma,
        dma,
        dma,
        dma((fields, wt)),
        dma((wt,)),
        dma((wt,)),
        dma((4,)),
        dma((4,)),
    ]
    return pl.pallas_call(
        functools.partial(kernel, (blocks_t, peers)),
        out_shape=jax.ShapeDtypeStruct(values.shape, values.dtype),
        in_specs=[
            pl.BlockSpec(memory_space=pltpu.HBM),
            pl.BlockSpec(memory_space=pltpu.VMEM),
            pl.BlockSpec(memory_space=pltpu.VMEM),
        ],
        out_specs=pl.BlockSpec(memory_space=pltpu.VMEM),
        scratch_shapes=scratch,
        compiler_params=pltpu.CompilerParams(
            collective_id=0,
            has_side_effects=True,
            vmem_limit_bytes=32 * 1024 * 1024,
        ),
    )(values, listed_from[None, :], listed_until[None, :])


def solution(mesh):
    in_specs = (P(None, "tm", "asset"), P("asset"), P("asset"))
    out_specs = P(None, "tm", "asset")
    body = functools.partial(per_device, mesh.shape["tm"], mesh.shape["asset"])
    return jax.shard_map(
        body, mesh=mesh, in_specs=in_specs, out_specs=out_specs, check_vma=False
    )
```

time: 118 us -> 72.7 us (0.62)
  Pallas kernels: 0 us -> 64.3 us
  waiting for transfers between devices: 53.6 us -> 0 us
  other arithmetic: 23.3 us -> 0 us
  matrix products: 20.4 us -> 0 us
  starting transfers between devices: 17.4 us -> 0 us
  local copies, waits for them, and re-layouts: 2.47 us -> 8.17 us
    pallas_call x0 -> x1, Pallas kernels: none -> 64.3 us  [per_device(): pl.pallas_call(functools.partial(kernel, (blocks_t, peers)), out_shape=ja...]
    ppermute x1 -> x0, waiting for transfers between devices: 36.1 us -> none  [passed_along(): return lax.ppermute(block, axis, route)]
    dot_general x3 -> x0, matrix products: 20.4 us -> none  [the longest x1 12.8 us: window_sums(): within = jnp.einsum('ij,fbja->fbia', lower_band, current, precision=highest)]
    all_to_all x2 -> x0, waiting for transfers between devices: 17.5 us -> none  [sent_to_all(): return lax.all_to_all(copies, axis, split_axis=0, concat_axis=0, tiled=True)]
    all_to_all x2 -> x0, starting transfers between devices: 13.3 us -> none  [sent_to_all(): return lax.all_to_all(copies, axis, split_axis=0, concat_axis=0, tiled=True)]
    unnamed x8 -> x7, local copies, waits for them, and re-layouts: 0.02 us -> 8.17 us
    reduce_sum x4 -> x0, other arithmetic: 7.38 us -> none  [the longest x1 6.55 us: standardize(): local_sum = jnp.sum(field_values * weight[None], axis=2)]
    div x3 -> x0, other arithmetic: 7.35 us -> none  [the longest x1 7.32 us: standardize(): return (deviate / jnp.sqrt(spread + 0.1)[:, :, None], count_total)]
  transfers between devices with their start and end apart: 3 -> 0, of which waited for: 3 -> 0; matrix products, arithmetic and copies ran while one was open for 8% -> 0% of each run, Pallas kernels for 0% -> 0%
where the time goes in v1:
time: 72.7 us; the launch traced here: 72.5 us
  Pallas kernels  64.3 us (88%)
  local copies, waits for them, and re-layouts  8.17 us (11%)
    pallas_call x1, Pallas kernels, per_device(): pl.pallas_call(functools.partial(kernel, (blocks_t, peers)), out_shape=ja...  64.3 us
    unnamed x7, local copies, waits for them, and re-layouts  8.17 us

profile of v1, /device:TPU:1, one launch (start us, length us, event | category | flops | bytes accessed | tf_op | source)
XLA Modules:
  0.0 72.5 jit_solution(5955627304971579023)
XLA Ops:
  0.0 0.0 copy-start
  0.0 3.4 %copy-done = f32[4,256,2048]{2,1,0:T(8,128)S(1)} copy-done((f32[4,256,2048]{2,1,0:T(8,128)S(1)}, f32[4,256,2048]{2,1,0:T(8,128)}, u32[]{:S(2)}) %copy-start) | copy-done | bytes 8388632
  3.4 0.0 copy-start.1
  3.4 0.7 copy-done.1
  4.1 0.0 copy-start.2
  4.1 0.7 copy-done.2
  4.8 64.3 %shard_map.37 = f32[4,256,2048]{2,1,0:T(8,128)S(1)} custom-call(f32[4,256,2048]{2,1,0:T(8,128)S(1)} %copy-done, s32[1,2048]{1,0:T(1,128)S(1)} %bitcast.2, s32[1,2048]{1,0:T(1,128)S(1)} %bitcast.3), custom_call_target="tpu_custom_call" | custom-call | tf_op jit(solution)/shard_map/pallas_call | solution.py:536
  69.1 3.4 %copy.5 = f32[4,256,2048]{2,1,0:T(8,128)} copy(f32[4,256,2048]{2,1,0:T(8,128)S(1)} %shard_map.37) | data formatting | bytes 16777216
Async XLA Ops:
  0.0 3.4 %copy-start = (f32[4,256,2048]{2,1,0:T(8,128)S(1)}, f32[4,256,2048]{2,1,0:T(8,128)}, u32[]{:S(2)}) copy-start(f32[4,256,2048]{2,1,0:T(8,128)} %vals.1) | copy-start | bytes 25165828
  3.4 0.7 copy-start.1
  4.1 0.7 copy-start.2

commit v2 on v1

v2 whole, which is shorter than its diff:
```python
import functools

import jax
import jax.numpy as jnp
from jax import lax
from jax.experimental import pallas as pl
from jax.experimental.pallas import tpu as pltpu
from jax.sharding import PartitionSpec as P

WINDOW = 64
TILE = 8
LANES = 128
CHUNK = 512
MESH = pl.DeviceIdType.MESH


def kernel(
    sizes,
    vals,
    opened_in,
    closed_in,
    out,
    opened,
    closed,
    list_sem,
    rounds,
    local_count,
    halo,
    hop1,
    hop2,
    ring,
    total,
    base,
    suffix,
    ahead,
    pivot,
    msg_b1,
    msg_b2,
    msg_g1,
    msg_g2,
    msg_h1,
    msg_h2,
    got_b1,
    got_b2,
    got_g1,
    got_g2,
    got_h1,
    got_h2,
    count_b,
    count_h,
    floor_b,
    floor_h,
    row_b1,
    row_b2,
    row_g1,
    row_g2,
    row_h1,
    row_h2,
    load_sem,
    direct_send,
    back_send,
    relay1_send,
    relay2_send,
    halo_recv,
    hop1_recv,
    hop2_recv,
    ex_send,
    ex_recv,
):
    blocks_t, peers = sizes
    fields, rows, assets = vals.shape
    tiles = rows // TILE
    wt = WINDOW // TILE
    chunks = assets // CHUNK
    bulk = tiles - wt
    back_field = fields - 1
    x = lax.axis_index("tm")
    me = lax.axis_index("asset")
    nxt = lax.rem(x + 1, blocks_t)
    prv = lax.rem(x + blocks_t - 1, blocks_t)
    t0 = x * rows

    dates = [
        pltpu.make_async_copy(opened_in, opened, list_sem.at[0]),
        pltpu.make_async_copy(closed_in, closed, list_sem.at[1]),
    ]
    for copy in dates:
        copy.start()

    def load(f, b):
        part = pl.ds(b * WINDOW, WINDOW)
        return pltpu.make_async_copy(
            vals.at[f, part, :], out.at[f, part, :], load_sem.at[f, b]
        )

    for b in range(rows // WINDOW):
        for f in range(fields):
            load(f, b).start()

    core = lax.rem(me, 2)
    chip = me // 2
    y, z = chip // 4, lax.rem(chip, 4)

    def at_place(dy, dz, dc):
        to = lax.rem(y + dy, 4) * 4 + lax.rem(z + dz, 4)
        return to * 2 + lax.rem(core + dc, 2)

    near = [at_place(0, 0, 1)]
    near += [at_place(1, 0, 0), at_place(3, 0, 0), at_place(0, 1, 0), at_place(0, 3, 0)]
    barrier = pltpu.get_barrier_semaphore()
    for t in (nxt, prv):
        pl.semaphore_signal(barrier, 1, device_id={"tm": t}, device_id_type=MESH)
    for peer in near:
        pl.semaphore_signal(barrier, 1, device_id={"asset": peer}, device_id_type=MESH)
    pl.semaphore_wait(barrier, 2 + len(near))

    def tell(i):
        for peer in near:
            pl.semaphore_signal(
                rounds.at[i], 1, device_id={"asset": peer}, device_id_type=MESH
            )

    def hear(i):
        pl.semaphore_wait(rounds.at[i], len(near))

    tell(0)

    tail = rows - WINDOW

    def tile_rows(r):
        return pl.ds(r * TILE, TILE)

    def direct(f, r):
        return pltpu.make_async_remote_copy(
            src_ref=vals.at[f, pl.ds(tail + r * TILE, TILE), :],
            dst_ref=halo.at[f, tile_rows(r), :],
            send_sem=direct_send,
            recv_sem=halo_recv.at[f, r],
            device_id={"tm": nxt},
            device_id_type=MESH,
        )

    def back(r):
        return pltpu.make_async_remote_copy(
            src_ref=vals.at[back_field, pl.ds(tail + r * TILE, TILE), :],
            dst_ref=hop1.at[tile_rows(r), :],
            send_sem=back_send,
            recv_sem=hop1_recv.at[r],
            device_id={"tm": prv},
            device_id_type=MESH,
        )

    def relay1(r):
        return pltpu.make_async_remote_copy(
            src_ref=hop1.at[tile_rows(r), :],
            dst_ref=hop2.at[tile_rows(r), :],
            send_sem=relay1_send,
            recv_sem=hop2_recv.at[r],
            device_id={"tm": prv},
            device_id_type=MESH,
        )

    def relay2(r):
        return pltpu.make_async_remote_copy(
            src_ref=hop2.at[tile_rows(r), :],
            dst_ref=halo.at[back_field, tile_rows(r), :],
            send_sem=relay2_send,
            recv_sem=halo_recv.at[back_field, r],
            device_id={"tm": prv},
            device_id_type=MESH,
        )

    has_next = x < blocks_t - 1
    order = list(range(wt - 1, -1, -1))

    @pl.when(has_next)
    def _():
        for r in order:
            back(r).start()
            for f in range(back_field):
                direct(f, r).start()

    def hops(d):
        return min(d[0], 4 - d[0]) + min(d[1], 4 - d[1]) + d[2] / 2

    places = [(dy, dz, dc) for dy in range(4) for dz in range(4) for dc in range(2)]
    places = sorted(places[1:], key=hops, reverse=True)

    def exchange(g, msg, got, k, peer):
        return pltpu.make_async_remote_copy(
            src_ref=msg,
            dst_ref=got.at[k],
            send_sem=ex_send.at[g],
            recv_sem=ex_recv.at[g],
            device_id={"asset": peer},
            device_id_type=MESH,
        )

    def exchange_start(g, msg, got):
        for d in places:
            k = (d[0] * 4 + d[1]) * 2 + d[2]
            exchange(g, msg, got, k, at_place(*d)).start()
        got[0] = msg[...]

    def exchange_all(g, got):
        others = got.at[pl.ds(1, peers - 1)]
        return pltpu.make_async_remote_copy(
            src_ref=others,
            dst_ref=others,
            send_sem=ex_send.at[g],
            recv_sem=ex_recv.at[g],
            device_id={"asset": me},
            device_id_type=MESH,
        )

    sub = lax.broadcasted_iota(jnp.int32, (TILE, LANES), 0)
    lane = lax.broadcasted_iota(jnp.int32, (TILE, LANES), 1)
    subc = lax.broadcasted_iota(jnp.int32, (TILE, CHUNK), 0)
    width = fields * TILE

    def lanes(c):
        return pl.ds(c * CHUNK, CHUNK)

    def fold(v):
        acc = v[:, :LANES]
        for i in range(1, CHUNK // LANES):
            acc = acc + v[:, i * LANES : (i + 1) * LANES]
        return acc

    def across(v):
        return jnp.sum(v, axis=1, keepdims=True)

    def flat(columns):
        z = jnp.zeros((TILE, LANES), jnp.float32)
        for at, column in columns:
            z = jnp.where(lane == sub + at, column, z)
        return jnp.sum(z, axis=0, keepdims=True)

    def column(row, at):
        return across(jnp.where(lane == sub + at, row, 0.0))

    def listed(c, first):
        t = subc + first
        o = opened[:, lanes(c)]
        u = closed[:, lanes(c)]
        return t, o, u, (t >= o) & (t < u)

    def share(t, o, u, w):
        low = jnp.maximum(jnp.maximum(t - (WINDOW - 1), o), 0)
        high = jnp.minimum(t, u - 1)
        counted = jnp.maximum(high - low + 1, 1).astype(jnp.float32)
        return jnp.where(w, 1.0 / counted, 0.0)

    def moments(count, s, q, pivots, which):
        inverse = 1.0 / jnp.maximum(count, 1.0)
        columns = []
        means = []
        for f, s_l, q_l, pivot_f in zip(which, s, q, pivots):
            s_f, q_f = across(s_l), across(q_l)
            lift = s_f * inverse
            mean = pivot_f + lift
            means.append(mean)
            columns.append((f * TILE, mean))
            columns.append((width + f * TILE, jnp.maximum(q_f - s_f * lift, 0.0)))
        return means, columns

    def counts_at(count, at):
        return [(at + f * TILE, count) for f in range(fields)]

    zero = jnp.zeros((TILE, LANES), jnp.float32)

    for copy in dates:
        copy.wait()
    msg_b1[...] = jnp.zeros_like(msg_b1)
    base[...] = jnp.zeros_like(base)
    for f in range(fields):
        load(f, 0).wait()

    def prefix(f, c, w, v):
        p = jnp.where(w, v, 0.0)
        for k in (1, 2, 4):
            p = p + jnp.where(subc >= k, pltpu.roll(p, k, 0), 0.0)
        p = p + base[f, :, lanes(c)]
        base[f, :, lanes(c)] = jnp.broadcast_to(p[TILE - 1 :, :], p.shape)
        return p

    def first_tile(r, carry):
        n = zero
        here = pl.ds(pl.multiple_of(r * TILE, TILE), TILE)
        for c in range(chunks):
            _, _, _, w = listed(c, t0 + r * TILE)
            n = n + fold(jnp.where(w, 1.0, 0.0))
            for f in range(fields):
                p = prefix(f, c, w, out[f, here, lanes(c)])
                ring[f, here, lanes(c)] = p
                out[f, here, lanes(c)] = p
        count = across(n)
        local_count[r] = jnp.broadcast_to(count, zero.shape)
        msg_b1[pl.ds(wt - 1 - r, 1), :] = flat(counts_at(count, 3 * width))
        return carry

    lax.fori_loop(0, wt, first_tile, 0)

    for f in range(fields):
        rough = zero
        for c in range(chunks):
            rough = rough + fold(base[f, :, lanes(c)])
        pivot[f] = jnp.broadcast_to(across(rough) * (1.0 / (WINDOW * assets)), zero.shape)

    every = list(range(fields))

    def bulk_tile(b, i, pivots):
        r = b * wt + i
        here = pl.ds(pl.multiple_of(r * TILE, TILE), TILE)
        slot = pl.ds(pl.multiple_of(i * TILE, TILE), TILE)
        n = zero
        s = [zero] * fields
        q = [zero] * fields
        for c in range(chunks):
            t, o, u, w = listed(c, t0 + r * TILE)
            n = n + fold(jnp.where(w, 1.0, 0.0))
            part = share(t, o, u, w)
            for f in range(fields):
                p = prefix(f, c, w, out[f, here, lanes(c)])
                old = ring[f, slot, lanes(c)]
                ring[f, slot, lanes(c)] = p
                rolled = (p + (total[f, :, lanes(c)] - old)) * part
                out[f, here, lanes(c)] = rolled
                d = jnp.where(w, rolled - pivots[f], 0.0)
                s[f] = s[f] + fold(d)
                q[f] = q[f] + fold(d * d)
        count = across(n)
        means, columns = moments(count, s, q, pivots, every)
        at = pl.ds(r - wt, 1)
        msg_b1[at, :] = msg_b1[at, :] + flat(columns + counts_at(count, 2 * width))
        return means

    def bulk_block(b):
        total[...] = base[...]
        base[...] = jnp.zeros_like(base)

        def pair(i, carry):
            pivots = [pivot[f][:, :1] for f in range(fields)]
            lower = bulk_tile(b, 2 * i, pivots)
            upper = bulk_tile(b, 2 * i + 1, pivots)
            for f in range(fields):
                pivot[f] = jnp.broadcast_to(upper[f], zero.shape)
            if b == 1:

                @pl.when(i == 0)
                def _():
                    for f in range(fields):
                        ahead[f] = jnp.broadcast_to(lower[f], zero.shape)

            return carry

        lax.fori_loop(0, wt // 2, pair, 0)

    for b in range(1, rows // WINDOW):
        hear(b - 1)
        tell(b)
        for f in range(fields):
            load(f, b).wait()
        bulk_block(b)
    hear(rows // WINDOW - 1)
    exchange_start(0, msg_b1, got_b1)

    @pl.when(x != blocks_t - 2)
    def _():
        for r in order:
            back(r).wait_recv()
            relay1(r).start()

    def scaled(center, spread):
        inv = 1.0 / jnp.sqrt(jnp.maximum(spread, 0.0) + 0.1)
        wide = lax.broadcasted_iota(jnp.int32, center.shape, 1)
        return jnp.where(wide < width, center, pltpu.roll(inv, width, 1))

    def left(v, by):
        return pltpu.roll(v, LANES - by, 1)

    def sum_over(term, shape):
        step = 8
        nothing = tuple(jnp.zeros(shape, jnp.float32) for _ in range(2))

        def some(i, acc):
            acc = list(acc)
            for j in range(step):
                acc[j % 2] = acc[j % 2] + term(i * step + j)
            return tuple(acc)

        if shape[0] == 1:
            acc = nothing
            for i in range(peers // step):
                acc = some(i, acc)
        else:
            acc = lax.fori_loop(0, peers // step, some, nothing)
        return acc[0] + acc[1]

    def merge(got, counts, floor, m2, rows_out):
        shape = rows_out.shape
        center = sum_over(lambda p: counts(p) * got[p], shape) / floor

        def spread_term(p):
            d = got[p] - center
            return counts(p) * d * d

        rows_out[...] = scaled(center, (sum_over(spread_term, shape) + m2) / floor)

    def summed(got):
        return sum_over(lambda p: got[p], got.shape[1:])

    def apply_tile(r, row, row_in, clipping):
        here = pl.ds(pl.multiple_of(r * TILE, TILE), TILE)
        line = jnp.broadcast_to(row_in[pl.ds(row, 1), :], zero.shape)
        center = [column(line, f * TILE) for f in range(fields)]
        inv = [column(line, width + f * TILE) for f in range(fields)]
        s = [zero] * fields
        q = [zero] * fields
        for c in range(chunks):
            _, _, _, w = listed(c, t0 + r * TILE)
            for f in range(fields):
                y = (out[f, here, lanes(c)] - center[f]) * inv[f]
                if clipping:
                    y = jnp.clip(y, -3.0, 3.0)
                y = jnp.where(w, y, 0.0)
                out[f, here, lanes(c)] = y
                if clipping:
                    s[f] = s[f] + fold(y)
                    q[f] = q[f] + fold(y * y)
        return s, q

    def clip_tile(r, row, row_in, msg, msg_row):
        s, q = apply_tile(r, row, row_in, True)
        columns = []
        for f in range(fields):
            columns.append((f * TILE, across(s[f])))
            columns.append((width + f * TILE, across(q[f])))
        msg[pl.ds(msg_row, 1), :] = flat(columns)

    def merge2(got, floor, rows_out):
        sums = summed(got)
        center = sums / floor
        spread = left(sums, width) / floor - center * center
        rows_out[...] = scaled(center, spread)

    def final_tile(r, row, row_in):
        apply_tile(r, row, row_in, False)

    def over(n, step, unroll=1):
        def one(i, carry):
            step(i)
            return carry

        lax.fori_loop(0, n, one, 0, unroll=unroll)

    def halo_part(r, which):
        here = tile_rows(r)

        @pl.when(x > 0)
        def _():
            for f in which:
                if f == back_field:
                    relay2(r).wait_recv()
                else:
                    direct(f, r).wait_recv()

        s = [zero] * len(which)
        q = [zero] * len(which)
        pivots = [ahead[f][:, :1] for f in which]
        for c in range(chunks):
            t, o, u, w = listed(c, t0 + r * TILE)
            _, _, _, past = listed(c, t0 + r * TILE - WINDOW)
            past = past & (t >= WINDOW)
            part = share(t, o, u, w)
            for i, f in enumerate(which):
                h = jnp.where(past, halo[f, here, lanes(c)], 0.0)
                for j in (1, 2, 4):
                    up = pltpu.roll(h, TILE - j, 0)
                    h = h + jnp.where(subc < TILE - j, up, 0.0)
                before = suffix[f, :, lanes(c)]
                after = jnp.where(subc < TILE - 1, pltpu.roll(h, TILE - 1, 0), 0.0)
                suffix[f, :, lanes(c)] = before + jnp.broadcast_to(h[:1, :], h.shape)
                rolled = (out[f, here, lanes(c)] + (before + after)) * part
                out[f, here, lanes(c)] = rolled
                d = jnp.where(w, rolled - pivots[i], 0.0)
                s[i] = s[i] + fold(d)
                q[i] = q[i] + fold(d * d)
        count = local_count[r][:, :1]
        means, columns = moments(count, s, q, pivots, which)
        for i, f in enumerate(which):
            ahead[f] = jnp.broadcast_to(means[i], zero.shape)
        line = flat(columns)
        if r == 0:
            at, msg = pl.ds(0, 1), msg_h1
        else:
            at, msg = pl.ds(wt - 1 - r, 1), msg_g1
        msg[at, :] = msg[at, :] + line

    suffix[...] = jnp.zeros_like(suffix)
    msg_h1[...] = jnp.zeros_like(msg_h1)
    msg_g1[...] = jnp.zeros_like(msg_g1)
    fore = every[:back_field]
    rear = [back_field]

    halo_part(7, fore)
    halo_part(6, fore)
    exchange_all(0, got_b1).wait_recv()

    def split(p):
        v = got_b1[p]
        count_b[p] = left(v, 2 * width)
        count_h[p] = left(v[:wt, :], 3 * width)

    over(peers, split, 8)
    sums = summed(got_b1)
    floor_b[...] = jnp.maximum(left(sums, 2 * width), 1.0)
    floor_h[...] = jnp.maximum(left(sums[:wt, :], 3 * width), 1.0)
    merge(got_b1, lambda p: count_b[p], floor_b[...], left(sums, width), row_b1)
    halo_part(5, fore)
    over(bulk, lambda i: clip_tile(i + wt, i, row_b1, msg_b2, i), 2)
    exchange_start(1, msg_b2, got_b2)
    halo_part(4, fore)

    @pl.when(x != blocks_t - 3)
    def _():
        for r in order:
            relay1(r).wait_recv()
            relay2(r).start()

    halo_part(3, fore)
    exchange_all(1, got_b2).wait_recv()
    merge2(got_b2, floor_b[...], row_b2)
    over(bulk, lambda i: final_tile(i + wt, i, row_b2), 2)
    halo_part(2, fore)
    for r in order[:5]:
        halo_part(r, rear)
    halo_part(1, fore)
    for r in order[5:7]:
        halo_part(r, rear)
    exchange_start(2, msg_g1, got_g1)
    halo_part(0, fore)
    halo_part(0, rear)
    exchange_start(3, msg_h1, got_h1)

    front = wt - 1
    exchange_all(2, got_g1).wait_recv()
    m2 = left(summed(got_g1), width)
    merge(got_g1, lambda p: count_h[p, :front, :], floor_h[:front, :], m2, row_g1)
    over(front, lambda i: clip_tile(front - i, i, row_g1, msg_g2, i), front)
    exchange_start(4, msg_g2, got_g2)
    exchange_all(3, got_h1).wait_recv()
    m2 = left(summed(got_h1), width)
    merge(got_h1, lambda p: count_h[p, front:, :], floor_h[front:, :], m2, row_h1)
    clip_tile(0, 0, row_h1, msg_h2, 0)
    exchange_start(5, msg_h2, got_h2)
    exchange_all(4, got_g2).wait_recv()
    merge2(got_g2, floor_h[:front, :], row_g2)
    over(front, lambda i: final_tile(front - i, i, row_g2), front)
    exchange_all(5, got_h2).wait_recv()
    merge2(got_h2, floor_h[front:, :], row_h2)
    final_tile(0, 0, row_h2)

    for g, got in enumerate((got_b1, got_b2, got_g1, got_h1, got_g2, got_h2)):
        exchange_all(g, got).wait_send()

    @pl.when(has_next)
    def _():
        for r in order:
            back(r).wait_send()
            for f in range(back_field):
                direct(f, r).wait_send()

    @pl.when(x != blocks_t - 2)
    def _():
        for r in order:
            relay1(r).wait_send()

    @pl.when(x != blocks_t - 3)
    def _():
        for r in order:
            relay2(r).wait_send()


def per_device(blocks_t, peers, values, listed_from, listed_until):
    fields, rows, assets = values.shape
    tiles = rows // TILE
    wt = WINDOW // TILE
    bulk = tiles - wt
    f32 = jnp.float32
    vmem = pltpu.VMEM
    dma = pltpu.SemaphoreType.DMA
    scratch = [
        vmem((1, assets), jnp.int32),
        vmem((1, assets), jnp.int32),
        dma((2,)),
        pltpu.SemaphoreType.REGULAR((4,)),
        vmem((wt, TILE, LANES), f32),
        vmem((fields, WINDOW, assets), f32),
        vmem((WINDOW, assets), f32),
        vmem((WINDOW, assets), f32),
        vmem((fields, WINDOW, assets), f32),
        vmem((fields, TILE, assets), f32),
        vmem((fields, TILE, assets), f32),
        vmem((fields, TILE, assets), f32),
        vmem((fields, TILE, LANES), f32),
        vmem((fields, TILE, LANES), f32),
        *[vmem((n, LANES), f32) for n in (bulk, bulk, wt - 1, wt - 1, 1, 1)],
        *[vmem((peers, n, LANES), f32) for n in (bulk, bulk, wt - 1, wt - 1, 1, 1)],
        *[vmem((peers, n, LANES), f32) for n in (bulk, wt)],
        *[vmem((n, LANES), f32) for n in (bulk, wt)],
        *[vmem((n, LANES), f32) for n in (bulk, bulk, wt - 1, wt - 1, 1, 1)],
        dma((fields, rows // WINDOW)),
        dma,
        dma,
        dma,
        dma,
        dma((fields, wt)),
        dma((wt,)),
        dma((wt,)),
        dma((6,)),
        dma((6,)),
    ]
    return pl.pallas_call(
        functools.partial(kernel, (blocks_t, peers)),
        out_shape=pltpu.VMEM(values.shape, values.dtype),
        in_specs=[
            pl.BlockSpec(memory_space=pltpu.HBM),
            pl.BlockSpec(memory_space=pltpu.HBM),
            pl.BlockSpec(memory_space=pltpu.HBM),
        ],
        out_specs=pl.BlockSpec(memory_space=pltpu.VMEM),
        scratch_shapes=scratch,
        compiler_params=pltpu.CompilerParams(
            collective_id=0,
            has_side_effects=True,
            vmem_limit_bytes=48 * 1024 * 1024,
        ),
    )(values, listed_from[None, :], listed_until[None, :])


def solution(mesh):
    in_specs = (P(None, "tm", "asset"), P("asset"), P("asset"))
    out_specs = P(None, "tm", "asset")
    body = functools.partial(per_device, mesh.shape["tm"], mesh.shape["asset"])
    return jax.shard_map(
        body, mesh=mesh, in_specs=in_specs, out_specs=out_specs, check_vma=False
    )
```

time: 72.7 us -> 56 us (0.77)
  the two profiles are of different devices: /device:TPU:1 before, /device:TPU:7 now
where the time goes in v2:
time: 56 us; the launch traced here: 55.9 us
  Pallas kernels  52.5 us (94%)
  local copies, waits for them, and re-layouts  3.4 us (6%)
    pallas_call x1, Pallas kernels, per_device(): pl.pallas_call(functools.partial(kernel, (blocks_t, peers)), out_shape=pl...  52.5 us
    unnamed x1, local copies, waits for them, and re-layouts  3.4 us

profile of v2, /device:TPU:7, one launch (start us, length us, event | category | flops | bytes accessed | tf_op | source)
XLA Modules:
  0.0 55.9 jit_solution(10714506255528237868)
XLA Ops:
  0.0 52.5 %shard_map.37 = f32[4,256,2048]{2,1,0:T(8,128)S(1)} custom-call(f32[4,256,2048]{2,1,0:T(8,128)} %vals.1, s32[1,2048]{1,0:T(1,128)} %bitcast.2, s32[1,2048]{1,0:T(1,128)} %bitcast.3), custom_call_target="tpu_custom_call" | custom-call | tf_op jit(solution)/shard_map/pallas_call | solution.py:624
  52.5 3.4 %copy.5 = f32[4,256,2048]{2,1,0:T(8,128)} copy(f32[4,256,2048]{2,1,0:T(8,128)S(1)} %shard_map.37) | data formatting | bytes 16777216

commit v3 on v2

--- a/solution.py
+++ b/solution.py
@@ -8,6 +8,8 @@
 from jax.sharding import PartitionSpec as P
 
 WINDOW = 64
+EARLY = 3
+LATE = 2
 TILE = 8
 LANES = 128
 CHUNK = 512
@@ -28,6 +30,9 @@
     halo,
     hop1,
     hop2,
+    ext,
+    params,
+    told,
     ring,
     total,
     base,
@@ -36,17 +41,18 @@
     pivot,
     msg_b1,
     msg_b2,
+    msg_e1,
+    msg_e2,
     msg_g1,
     msg_g2,
-    msg_h1,
-    msg_h2,
     got_b1,
     got_b2,
+    got_e1,
+    got_e2,
     got_g1,
     got_g2,
-    got_h1,
-    got_h2,
     count_b,
+    count_e,
     count_h,
     floor_b,
     floor_h,
@@ -54,10 +60,12 @@
     row_b2,
     row_g1,
     row_g2,
-    row_h1,
-    row_h2,
     load_sem,
     direct_send,
+    ext_send,
+    ext_recv,
+    told_send,
+    told_recv,
     back_send,
     relay1_send,
     relay2_send,
@@ -73,7 +81,6 @@
     wt = WINDOW // TILE
     chunks = assets // CHUNK
     bulk = tiles - wt
-    back_field = fields - 1
     x = lax.axis_index("tm")
     me = lax.axis_index("asset")
     nxt = lax.rem(x + 1, blocks_t)
@@ -129,6 +136,10 @@
 
     def tile_rows(r):
         return pl.ds(r * TILE, TILE)
+
+    every = list(range(fields))
+    fore, rear = every[: fields - LATE], every[fields - LATE :]
+    around = [(f, r) for r in range(EARLY - 1, -1, -1) for f in rear]
 
     def direct(f, r):
         return pltpu.make_async_remote_copy(
@@ -140,45 +151,84 @@
             device_id_type=MESH,
         )
 
-    def back(r):
+    def back(k):
+        f, r = around[k]
         return pltpu.make_async_remote_copy(
-            src_ref=vals.at[back_field, pl.ds(tail + r * TILE, TILE), :],
-            dst_ref=hop1.at[tile_rows(r), :],
+            src_ref=vals.at[f, pl.ds(tail + r * TILE, TILE), :],
+            dst_ref=hop1.at[tile_rows(k), :],
             send_sem=back_send,
-            recv_sem=hop1_recv.at[r],
+            recv_sem=hop1_recv.at[k],
             device_id={"tm": prv},
             device_id_type=MESH,
         )
 
-    def relay1(r):
+    def relay1(k):
         return pltpu.make_async_remote_copy(
-            src_ref=hop1.at[tile_rows(r), :],
-            dst_ref=hop2.at[tile_rows(r), :],
+            src_ref=hop1.at[tile_rows(k), :],
+            dst_ref=hop2.at[tile_rows(k), :],
             send_sem=relay1_send,
-            recv_sem=hop2_recv.at[r],
+            recv_sem=hop2_recv.at[k],
             device_id={"tm": prv},
             device_id_type=MESH,
         )
 
-    def relay2(r):
+    def relay2(k):
+        f, r = around[k]
         return pltpu.make_async_remote_copy(
-            src_ref=hop2.at[tile_rows(r), :],
-            dst_ref=halo.at[back_field, tile_rows(r), :],
+            src_ref=hop2.at[tile_rows(k), :],
+            dst_ref=halo.at[f, tile_rows(r), :],
             send_sem=relay2_send,
-            recv_sem=halo_recv.at[back_field, r],
+            recv_sem=halo_recv.at[f, r],
             device_id={"tm": prv},
             device_id_type=MESH,
         )
 
+    def pass1(ks):
+        for k in ks:
+            back(k).wait_recv()
+            relay1(k).start()
+
+    def pass2(ks):
+        for k in ks:
+            relay1(k).wait_recv()
+            relay2(k).start()
+
+    extension = pltpu.make_async_remote_copy(
+        src_ref=vals.at[:, pl.ds(0, EARLY * TILE), :],
+        dst_ref=ext,
+        send_sem=ext_send,
+        recv_sem=ext_recv,
+        device_id={"tm": prv},
+        device_id_type=MESH,
+    )
+    telling = pltpu.make_async_remote_copy(
+        src_ref=params,
+        dst_ref=told,
+        send_sem=told_send,
+        recv_sem=told_recv,
+        device_id={"tm": nxt},
+        device_id_type=MESH,
+    )
+
+    has_prev = x > 0
     has_next = x < blocks_t - 1
-    order = list(range(wt - 1, -1, -1))
+    last = x == blocks_t - 1
+    hops1 = x != blocks_t - 2
+    hops2 = x != blocks_t - 3
+    straight = [
+        (f, r) for r in range(wt - 1, -1, -1) for f in every if (f, r) not in around
+    ]
+
+    @pl.when(has_prev)
+    def _():
+        extension.start()
 
     @pl.when(has_next)
     def _():
-        for r in order:
-            back(r).start()
-            for f in range(back_field):
-                direct(f, r).start()
+        for k in range(len(around)):
+            back(k).start()
+        for f, r in straight:
+            direct(f, r).start()
 
     def hops(d):
         return min(d[0], 4 - d[0]) + min(d[1], 4 - d[1]) + d[2] / 2
@@ -307,32 +357,34 @@
             rough = rough + fold(base[f, :, lanes(c)])
         pivot[f] = jnp.broadcast_to(across(rough) * (1.0 / (WINDOW * assets)), zero.shape)
 
-    every = list(range(fields))
-
-    def bulk_tile(b, i, pivots):
-        r = b * wt + i
-        here = pl.ds(pl.multiple_of(r * TILE, TILE), TILE)
+    def window_tile(ref, here, first, i, pivots):
         slot = pl.ds(pl.multiple_of(i * TILE, TILE), TILE)
         n = zero
         s = [zero] * fields
         q = [zero] * fields
         for c in range(chunks):
-            t, o, u, w = listed(c, t0 + r * TILE)
+            t, o, u, w = listed(c, first)
             n = n + fold(jnp.where(w, 1.0, 0.0))
             part = share(t, o, u, w)
             for f in range(fields):
-                p = prefix(f, c, w, out[f, here, lanes(c)])
+                p = prefix(f, c, w, ref[f, here, lanes(c)])
                 old = ring[f, slot, lanes(c)]
                 ring[f, slot, lanes(c)] = p
                 rolled = (p + (total[f, :, lanes(c)] - old)) * part
-                out[f, here, lanes(c)] = rolled
+                ref[f, here, lanes(c)] = rolled
                 d = jnp.where(w, rolled - pivots[f], 0.0)
                 s[f] = s[f] + fold(d)
                 q[f] = q[f] + fold(d * d)
         count = across(n)
         means, columns = moments(count, s, q, pivots, every)
+        return means, flat(columns + counts_at(count, 2 * width))
+
+    def bulk_tile(b, i, pivots):
+        r = b * wt + i
+        here = pl.ds(pl.multiple_of(r * TILE, TILE), TILE)
+        means, line = window_tile(out, here, t0 + r * TILE, i, pivots)
         at = pl.ds(r - wt, 1)
-        msg_b1[at, :] = msg_b1[at, :] + flat(columns + counts_at(count, 2 * width))
+        msg_b1[at, :] = msg_b1[at, :] + line
         return means
 
     def bulk_block(b):
@@ -365,11 +417,10 @@
     hear(rows // WINDOW - 1)
     exchange_start(0, msg_b1, got_b1)
 
-    @pl.when(x != blocks_t - 2)
-    def _():
-        for r in order:
-            back(r).wait_recv()
-            relay1(r).start()
+
+    @pl.when(last)
+    def _():
+        pass1(range(len(around)))
 
     def scaled(center, spread):
         inv = 1.0 / jnp.sqrt(jnp.maximum(spread, 0.0) + 0.1)
@@ -389,7 +440,7 @@
                 acc[j % 2] = acc[j % 2] + term(i * step + j)
             return tuple(acc)
 
-        if shape[0] == 1:
+        if shape[0] <= TILE:
             acc = nothing
             for i in range(peers // step):
                 acc = some(i, acc)
@@ -410,28 +461,30 @@
     def summed(got):
         return sum_over(lambda p: got[p], got.shape[1:])
 
-    def apply_tile(r, row, row_in, clipping):
+    def apply_tile(ref, r, row, row_in, clipping, keep=True):
         here = pl.ds(pl.multiple_of(r * TILE, TILE), TILE)
+        first = t0 + r * TILE if ref is out else t0 + rows + r * TILE
         line = jnp.broadcast_to(row_in[pl.ds(row, 1), :], zero.shape)
         center = [column(line, f * TILE) for f in range(fields)]
         inv = [column(line, width + f * TILE) for f in range(fields)]
         s = [zero] * fields
         q = [zero] * fields
         for c in range(chunks):
-            _, _, _, w = listed(c, t0 + r * TILE)
+            _, _, _, w = listed(c, first)
             for f in range(fields):
-                y = (out[f, here, lanes(c)] - center[f]) * inv[f]
+                y = (ref[f, here, lanes(c)] - center[f]) * inv[f]
                 if clipping:
                     y = jnp.clip(y, -3.0, 3.0)
                 y = jnp.where(w, y, 0.0)
-                out[f, here, lanes(c)] = y
+                if keep:
+                    ref[f, here, lanes(c)] = y
                 if clipping:
                     s[f] = s[f] + fold(y)
                     q[f] = q[f] + fold(y * y)
         return s, q
 
-    def clip_tile(r, row, row_in, msg, msg_row):
-        s, q = apply_tile(r, row, row_in, True)
+    def clip_tile(ref, r, row, row_in, msg, msg_row):
+        s, q = apply_tile(ref, r, row, row_in, True, ref is out)
         columns = []
         for f in range(fields):
             columns.append((f * TILE, across(s[f])))
@@ -445,7 +498,7 @@
         rows_out[...] = scaled(center, spread)
 
     def final_tile(r, row, row_in):
-        apply_tile(r, row, row_in, False)
+        apply_tile(out, r, row, row_in, False)
 
     def over(n, step, unroll=1):
         def one(i, carry):
@@ -454,57 +507,90 @@
 
         lax.fori_loop(0, n, one, 0, unroll=unroll)
 
-    def halo_part(r, which):
+    def arrival(f, r):
+        k = around.index((f, r)) if (f, r) in around else None
+        return direct(f, r) if k is None else relay2(k)
+
+    def joined(f, c, here, past):
+        h = jnp.where(past, halo[f, here, lanes(c)], 0.0)
+        for j in (1, 2, 4):
+            up = pltpu.roll(h, TILE - j, 0)
+            h = h + jnp.where(subc < TILE - j, up, 0.0)
+        before = suffix[f, :, lanes(c)]
+        after = jnp.where(subc < TILE - 1, pltpu.roll(h, TILE - 1, 0), 0.0)
+        suffix[f, :, lanes(c)] = before + jnp.broadcast_to(h[:1, :], h.shape)
+        return out[f, here, lanes(c)] + (before + after)
+
+    def before_mask(c, t, r):
+        _, _, _, past = listed(c, t0 + r * TILE - WINDOW)
+        return past & (t >= WINDOW)
+
+    def halo_part(r, msg, row, extra):
         here = tile_rows(r)
-
-        @pl.when(x > 0)
-        def _():
-            for f in which:
-                if f == back_field:
-                    relay2(r).wait_recv()
-                else:
-                    direct(f, r).wait_recv()
-
-        s = [zero] * len(which)
-        q = [zero] * len(which)
-        pivots = [ahead[f][:, :1] for f in which]
+        s = [zero] * fields
+        q = [zero] * fields
+        pivots = [ahead[f][:, :1] for f in every]
         for c in range(chunks):
             t, o, u, w = listed(c, t0 + r * TILE)
-            _, _, _, past = listed(c, t0 + r * TILE - WINDOW)
-            past = past & (t >= WINDOW)
+            past = before_mask(c, t, r)
+            part = share(t, o, u, w)
+            for f in every:
+                rolled = joined(f, c, here, past) * part
+                out[f, here, lanes(c)] = rolled
+                d = jnp.where(w, rolled - pivots[f], 0.0)
+                s[f] = s[f] + fold(d)
+                q[f] = q[f] + fold(d * d)
+        count = local_count[r][:, :1]
+        means, columns = moments(count, s, q, pivots, every)
+        for f in every:
+            ahead[f] = jnp.broadcast_to(means[f], zero.shape)
+        if extra:
+            columns = columns + counts_at(count, 2 * width)
+        msg[pl.ds(row, 1), :] = flat(columns)
+
+    def group_tile(r):
+        @pl.when(has_prev)
+        def _():
+            for f in every:
+                arrival(f, r).wait_recv()
+
+        halo_part(r, msg_g1, wt - 1 - r, False)
+
+    def finish(r, which):
+        here = tile_rows(r)
+        lines = [jnp.broadcast_to(told[i, pl.ds(r, 1), :], zero.shape) for i in range(2)]
+        center = [[column(line, f * TILE) for f in which] for line in lines]
+        inv = [[column(line, width + f * TILE) for f in which] for line in lines]
+        for f in which:
+            arrival(f, r).wait_recv()
+        for c in range(chunks):
+            t, o, u, w = listed(c, t0 + r * TILE)
+            past = before_mask(c, t, r)
             part = share(t, o, u, w)
             for i, f in enumerate(which):
-                h = jnp.where(past, halo[f, here, lanes(c)], 0.0)
-                for j in (1, 2, 4):
-                    up = pltpu.roll(h, TILE - j, 0)
-                    h = h + jnp.where(subc < TILE - j, up, 0.0)
-                before = suffix[f, :, lanes(c)]
-                after = jnp.where(subc < TILE - 1, pltpu.roll(h, TILE - 1, 0), 0.0)
-                suffix[f, :, lanes(c)] = before + jnp.broadcast_to(h[:1, :], h.shape)
-                rolled = (out[f, here, lanes(c)] + (before + after)) * part
-                out[f, here, lanes(c)] = rolled
-                d = jnp.where(w, rolled - pivots[i], 0.0)
-                s[i] = s[i] + fold(d)
-                q[i] = q[i] + fold(d * d)
-        count = local_count[r][:, :1]
-        means, columns = moments(count, s, q, pivots, which)
-        for i, f in enumerate(which):
-            ahead[f] = jnp.broadcast_to(means[i], zero.shape)
-        line = flat(columns)
-        if r == 0:
-            at, msg = pl.ds(0, 1), msg_h1
-        else:
-            at, msg = pl.ds(wt - 1 - r, 1), msg_g1
-        msg[at, :] = msg[at, :] + line
+                rolled = joined(f, c, here, past) * part
+                y = jnp.clip((rolled - center[0][i]) * inv[0][i], -3.0, 3.0)
+                y = (y - center[1][i]) * inv[1][i]
+                out[f, here, lanes(c)] = jnp.where(w, y, 0.0)
 
     suffix[...] = jnp.zeros_like(suffix)
-    msg_h1[...] = jnp.zeros_like(msg_h1)
-    msg_g1[...] = jnp.zeros_like(msg_g1)
-    fore = every[:back_field]
-    rear = [back_field]
-
-    halo_part(7, fore)
-    halo_part(6, fore)
+    msg_e1[...] = jnp.zeros_like(msg_e1)
+    msg_e2[...] = jnp.zeros_like(msg_e2)
+
+
+    def second(ks):
+        @pl.when((x == 0) | last)
+        def _():
+            pass2(ks)
+
+    group_tile(7)
+    group_tile(6)
+
+    @pl.when(x == 0)
+    def _():
+        for r in range(EARLY - 1, -1, -1):
+            halo_part(r, msg_e1, EARLY + r, True)
+
     exchange_all(0, got_b1).wait_recv()
 
     def split(p):
@@ -517,69 +603,142 @@
     floor_b[...] = jnp.maximum(left(sums, 2 * width), 1.0)
     floor_h[...] = jnp.maximum(left(sums[:wt, :], 3 * width), 1.0)
     merge(got_b1, lambda p: count_b[p], floor_b[...], left(sums, width), row_b1)
-    halo_part(5, fore)
-    over(bulk, lambda i: clip_tile(i + wt, i, row_b1, msg_b2, i), 2)
+    group_tile(5)
+
+    @pl.when(has_next)
+    def _():
+        total[...] = base[...]
+        base[...] = jnp.zeros_like(base)
+        extension.wait_recv()
+
+        def one(r, carry):
+            here = pl.ds(pl.multiple_of(r * TILE, TILE), TILE)
+            pivots = [pivot[f][:, :1] for f in every]
+            means, line = window_tile(ext, here, t0 + rows + r * TILE, r, pivots)
+            for f in every:
+                pivot[f] = jnp.broadcast_to(means[f], zero.shape)
+            msg_e1[pl.ds(r, 1), :] = line
+            return carry
+
+        lax.fori_loop(0, EARLY, one, 0)
+
+    exchange_start(2, msg_e1, got_e1)
+    over(bulk, lambda i: clip_tile(out, i + wt, i, row_b1, msg_b2, i), 2)
     exchange_start(1, msg_b2, got_b2)
-    halo_part(4, fore)
-
-    @pl.when(x != blocks_t - 3)
-    def _():
-        for r in order:
-            relay1(r).wait_recv()
-            relay2(r).start()
-
-    halo_part(3, fore)
+    some = range(4)
+
+    @pl.when(x < blocks_t - 2)
+    def _():
+        pass1(some)
+
+    @pl.when(x == blocks_t - 2)
+    def _():
+        pass2(some)
+
+    exchange_all(2, got_e1).wait_recv()
+
+    def split_e(p):
+        count_e[p] = left(got_e1[p], 2 * width)
+
+    over(peers, split_e, peers)
+    sums = summed(got_e1)
+    floor_e = jnp.maximum(left(sums, 2 * width), 1.0)
+    first_params, second_params = params.at[0], params.at[1]
+    merge(got_e1, lambda p: count_e[p], floor_e, left(sums, width), first_params)
+
+    @pl.when(has_next)
+    def _():
+        over(EARLY, lambda r: clip_tile(ext, r, r, first_params, msg_e2, r))
+
+    @pl.when(x == 0)
+    def _():
+        over(
+            EARLY,
+            lambda r: clip_tile(out, r, EARLY + r, first_params, msg_e2, EARLY + r),
+        )
+
+    exchange_start(3, msg_e2, got_e2)
+    group_tile(4)
+    rest = range(4, len(around))
+
+    @pl.when(x < blocks_t - 2)
+    def _():
+        pass1(rest)
+
+    @pl.when(x == blocks_t - 2)
+    def _():
+        pass2(rest)
+
+    second([0])
+    group_tile(3)
+    exchange_start(4, msg_g1, got_g1)
+    second([1])
+    exchange_all(3, got_e2).wait_recv()
+    merge2(got_e2, floor_e, second_params)
+
+    @pl.when(has_next)
+    def _():
+        telling.start()
+
+
+    @pl.when(x == 0)
+    def _():
+        over(EARLY, lambda r: final_tile(r, EARLY + r, second_params))
+
+    second([2,3])
+    front = wt - EARLY
+    exchange_all(4, got_g1).wait_recv()
+    second([4])
+    m2 = left(summed(got_g1), width)
+    merge(got_g1, lambda p: count_h[p, :front, :], floor_h[:front, :], m2, row_g1)
+    over(front, lambda i: clip_tile(out, wt - 1 - i, i, row_g1, msg_g2, i), front)
+    exchange_start(5, msg_g2, got_g2)
+    second([5])
     exchange_all(1, got_b2).wait_recv()
     merge2(got_b2, floor_b[...], row_b2)
     over(bulk, lambda i: final_tile(i + wt, i, row_b2), 2)
-    halo_part(2, fore)
-    for r in order[:5]:
-        halo_part(r, rear)
-    halo_part(1, fore)
-    for r in order[5:7]:
-        halo_part(r, rear)
-    exchange_start(2, msg_g1, got_g1)
-    halo_part(0, fore)
-    halo_part(0, rear)
-    exchange_start(3, msg_h1, got_h1)
-
-    front = wt - 1
-    exchange_all(2, got_g1).wait_recv()
-    m2 = left(summed(got_g1), width)
-    merge(got_g1, lambda p: count_h[p, :front, :], floor_h[:front, :], m2, row_g1)
-    over(front, lambda i: clip_tile(front - i, i, row_g1, msg_g2, i), front)
-    exchange_start(4, msg_g2, got_g2)
-    exchange_all(3, got_h1).wait_recv()
-    m2 = left(summed(got_h1), width)
-    merge(got_h1, lambda p: count_h[p, front:, :], floor_h[front:, :], m2, row_h1)
-    clip_tile(0, 0, row_h1, msg_h2, 0)
-    exchange_start(5, msg_h2, got_h2)
-    exchange_all(4, got_g2).wait_recv()
+
+
+    @pl.when(has_prev)
+    def _():
+        telling.wait_recv()
+
+
+    @pl.when(has_prev)
+    def _():
+        for r in range(EARLY - 1, -1, -1):
+            finish(r, fore)
+        for r in range(EARLY - 1, -1, -1):
+            finish(r, rear)
+
+    exchange_all(5, got_g2).wait_recv()
     merge2(got_g2, floor_h[:front, :], row_g2)
-    over(front, lambda i: final_tile(front - i, i, row_g2), front)
-    exchange_all(5, got_h2).wait_recv()
-    merge2(got_h2, floor_h[front:, :], row_h2)
-    final_tile(0, 0, row_h2)
-
-    for g, got in enumerate((got_b1, got_b2, got_g1, got_h1, got_g2, got_h2)):
+    over(front, lambda i: final_tile(wt - 1 - i, i, row_g2), front)
+
+    for g, got in enumerate((got_b1, got_b2, got_e1, got_e2, got_g1, got_g2)):
         exchange_all(g, got).wait_send()
 
+    @pl.when(has_prev)
+    def _():
+        extension.wait_send()
+
     @pl.when(has_next)
     def _():
-        for r in order:
-            back(r).wait_send()
-            for f in range(back_field):
-                direct(f, r).wait_send()
-
-    @pl.when(x != blocks_t - 2)
-    def _():
-        for r in order:
-            relay1(r).wait_send()
-
-    @pl.when(x != blocks_t - 3)
-    def _():
-        for r in order:
-            relay2(r).wait_send()
+        telling.wait_send()
+        for k in range(len(around)):
+            back(k).wait_send()
+        for f, r in straight:
+            direct(f, r).wait_send()
+
+    @pl.when(hops1)
+    def _():
+        for k in range(len(around)):
+            relay1(k).wait_send()
+
+    @pl.when(hops2)
+    def _():
+        for k in range(len(around)):
+            relay2(k).wait_send()
 
 
 def per_device(blocks_t, peers, values, listed_from, listed_until):
@@ -590,6 +749,8 @@
     f32 = jnp.float32
     vmem = pltpu.VMEM
     dma = pltpu.SemaphoreType.DMA
+    around = EARLY * LATE
+    groups = (bulk, bulk, 2 * EARLY, 2 * EARLY, wt - EARLY, wt - EARLY)
     scratch = [
         vmem((1, assets), jnp.int32),
         vmem((1, assets), jnp.int32),
@@ -597,27 +758,34 @@
         pltpu.SemaphoreType.REGULAR((4,)),
         vmem((wt, TILE, LANES), f32),
         vmem((fields, WINDOW, assets), f32),
-        vmem((WINDOW, assets), f32),
-        vmem((WINDOW, assets), f32),
+        vmem((around * TILE, assets), f32),
+        vmem((around * TILE, assets), f32),
+        vmem((fields, EARLY * TILE, assets), f32),
+        vmem((2, 2 * EARLY, LANES), f32),
+        vmem((2, 2 * EARLY, LANES), f32),
         vmem((fields, WINDOW, assets), f32),
         vmem((fields, TILE, assets), f32),
         vmem((fields, TILE, assets), f32),
         vmem((fields, TILE, assets), f32),
         vmem((fields, TILE, LANES), f32),
         vmem((fields, TILE, LANES), f32),
-        *[vmem((n, LANES), f32) for n in (bulk, bulk, wt - 1, wt - 1, 1, 1)],
-        *[vmem((peers, n, LANES), f32) for n in (bulk, bulk, wt - 1, wt - 1, 1, 1)],
-        *[vmem((peers, n, LANES), f32) for n in (bulk, wt)],
+        *[vmem((n, LANES), f32) for n in groups],
+        *[vmem((peers, n, LANES), f32) for n in groups],
+        *[vmem((peers, n, LANES), f32) for n in (bulk, 2 * EARLY, wt)],
         *[vmem((n, LANES), f32) for n in (bulk, wt)],
-        *[vmem((n, LANES), f32) for n in (bulk, bulk, wt - 1, wt - 1, 1, 1)],
+        *[vmem((n, LANES), f32) for n in (bulk, bulk, wt - EARLY, wt - EARLY)],
         dma((fields, rows // WINDOW)),
         dma,
         dma,
         dma,
         dma,
+        dma,
+        dma,
+        dma,
+        dma,
         dma((fields, wt)),
-        dma((wt,)),
-        dma((wt,)),
+        dma((around,)),
+        dma((around,)),
         dma((6,)),
         dma((6,)),
     ]

time: 56 us -> 51.6 us (0.921)
  the two profiles are of different devices: /device:TPU:7 before, /device:TPU:1 now
where the time goes in v3:
time: 51.6 us; the launch traced here: 51.5 us
  Pallas kernels  48.1 us (93%)
  local copies, waits for them, and re-layouts  3.4 us (7%)
    pallas_call x1, Pallas kernels, per_device(): pl.pallas_call(functools.partial(kernel, (blocks_t, peers)), out_shape=pl...  48.1 us
    unnamed x1, local copies, waits for them, and re-layouts  3.4 us

profile of v3, /device:TPU:1, one launch (start us, length us, event | category | flops | bytes accessed | tf_op | source)
XLA Modules:
  0.0 51.5 jit_solution(366982834816163478)
XLA Ops:
  0.0 48.1 %shard_map.37 = f32[4,256,2048]{2,1,0:T(8,128)S(1)} custom-call(f32[4,256,2048]{2,1,0:T(8,128)} %vals.1, s32[1,2048]{1,0:T(1,128)} %bitcast.2, s32[1,2048]{1,0:T(1,128)} %bitcast.3), custom_call_target="tpu_custom_call" | custom-call | tf_op jit(solution)/shard_map/pallas_call | solution.py:792
  48.1 3.4 %copy.5 = f32[4,256,2048]{2,1,0:T(8,128)} copy(f32[4,256,2048]{2,1,0:T(8,128)S(1)} %shard_map.37) | data formatting | bytes 16777216

commit v4 on v3

--- a/solution.py
+++ b/solution.py
@@ -9,7 +9,10 @@
 
 WINDOW = 64
 EARLY = 3
-LATE = 2
+BACK = ((3, 2), (3, 1), (2, 1), (3, 0), (2, 0))
+EXTRA = 1
+HALVES = 2
+MARK = 4.0
 TILE = 8
 LANES = 128
 CHUNK = 512
@@ -59,7 +62,6 @@
     row_b1,
     row_b2,
     row_g1,
-    row_g2,
     load_sem,
     direct_send,
     ext_send,
@@ -70,6 +72,7 @@
     relay1_send,
     relay2_send,
     halo_recv,
+    back_recv,
     hop1_recv,
     hop2_recv,
     ex_send,
@@ -94,15 +97,14 @@
     for copy in dates:
         copy.start()
 
-    def load(f, b):
+    def load(b):
         part = pl.ds(b * WINDOW, WINDOW)
         return pltpu.make_async_copy(
-            vals.at[f, part, :], out.at[f, part, :], load_sem.at[f, b]
+            vals.at[:, part, :], out.at[:, part, :], load_sem.at[b]
         )
 
     for b in range(rows // WINDOW):
-        for f in range(fields):
-            load(f, b).start()
+        load(b).start()
 
     core = lax.rem(me, 2)
     chip = me // 2
@@ -138,23 +140,48 @@
         return pl.ds(r * TILE, TILE)
 
     every = list(range(fields))
-    fore, rear = every[: fields - LATE], every[fields - LATE :]
-    around = [(f, r) for r in range(EARLY - 1, -1, -1) for f in rear]
-
-    def direct(f, r):
+    kept, extra = every[: fields - EXTRA], every[fields - EXTRA :]
+    tops = EARLY + (1 if EXTRA else 0)
+    piece = assets // HALVES
+    tiles_back = sorted({r for _, r in BACK}, reverse=True)
+    around = [
+        (f, r, h) for t in tiles_back for h in range(HALVES) for f, r in BACK if r == t
+    ]
+
+    def early(r):
+        return every if r < EARLY else extra
+
+    def grouped(r):
+        return every if r > EARLY else kept
+
+    def half(h):
+        return pl.ds(h * piece, piece)
+
+    straight = []
+    for r in range(wt - 1, -1, -1):
+        left_over = [f for f in every if (f, r) not in BACK]
+        if r == EARLY:
+            cuts = [kept[:-1], kept[-1:], extra]
+        else:
+            cuts = [left_over]
+        straight.extend((r, cut) for cut in cuts if cut)
+
+    def direct(i):
+        r, cut = straight[i]
+        which = pl.ds(cut[0], len(cut))
         return pltpu.make_async_remote_copy(
-            src_ref=vals.at[f, pl.ds(tail + r * TILE, TILE), :],
-            dst_ref=halo.at[f, tile_rows(r), :],
+            src_ref=vals.at[which, pl.ds(tail + r * TILE, TILE), :],
+            dst_ref=halo.at[which, tile_rows(r), :],
             send_sem=direct_send,
-            recv_sem=halo_recv.at[f, r],
+            recv_sem=halo_recv.at[i],
             device_id={"tm": nxt},
             device_id_type=MESH,
         )
 
     def back(k):
-        f, r = around[k]
+        f, r, h = around[k]
         return pltpu.make_async_remote_copy(
-            src_ref=vals.at[f, pl.ds(tail + r * TILE, TILE), :],
+            src_ref=vals.at[f, pl.ds(tail + r * TILE, TILE), half(h)],
             dst_ref=hop1.at[tile_rows(k), :],
             send_sem=back_send,
             recv_sem=hop1_recv.at[k],
@@ -173,12 +200,12 @@
         )
 
     def relay2(k):
-        f, r = around[k]
+        f, r, h = around[k]
         return pltpu.make_async_remote_copy(
             src_ref=hop2.at[tile_rows(k), :],
-            dst_ref=halo.at[f, tile_rows(r), :],
+            dst_ref=halo.at[f, tile_rows(r), half(h)],
             send_sem=relay2_send,
-            recv_sem=halo_recv.at[f, r],
+            recv_sem=back_recv.at[k],
             device_id={"tm": prv},
             device_id_type=MESH,
         )
@@ -193,14 +220,19 @@
             relay1(k).wait_recv()
             relay2(k).start()
 
-    extension = pltpu.make_async_remote_copy(
-        src_ref=vals.at[:, pl.ds(0, EARLY * TILE), :],
-        dst_ref=ext,
-        send_sem=ext_send,
-        recv_sem=ext_recv,
-        device_id={"tm": prv},
-        device_id_type=MESH,
-    )
+    def extension(i):
+        which = (pl.ds(0, fields), pl.ds(fields - EXTRA, EXTRA))[i]
+        part = (pl.ds(0, EARLY * TILE), pl.ds(EARLY * TILE, TILE))[i]
+        return pltpu.make_async_remote_copy(
+            src_ref=vals.at[which, part, :],
+            dst_ref=ext.at[which, part, :],
+            send_sem=ext_send.at[i],
+            recv_sem=ext_recv.at[i],
+            device_id={"tm": prv},
+            device_id_type=MESH,
+        )
+
+    extensions = [extension(i) for i in range(2 if EXTRA else 1)]
     telling = pltpu.make_async_remote_copy(
         src_ref=params,
         dst_ref=told,
@@ -215,20 +247,17 @@
     last = x == blocks_t - 1
     hops1 = x != blocks_t - 2
     hops2 = x != blocks_t - 3
-    straight = [
-        (f, r) for r in range(wt - 1, -1, -1) for f in every if (f, r) not in around
-    ]
-
     @pl.when(has_prev)
     def _():
-        extension.start()
+        for copy in extensions:
+            copy.start()
 
     @pl.when(has_next)
     def _():
         for k in range(len(around)):
             back(k).start()
-        for f, r in straight:
-            direct(f, r).start()
+        for i in range(len(straight) - 1):
+            direct(i).start()
 
     def hops(d):
         return min(d[0], 4 - d[0]) + min(d[1], 4 - d[1]) + d[2] / 2
@@ -323,8 +352,7 @@
         copy.wait()
     msg_b1[...] = jnp.zeros_like(msg_b1)
     base[...] = jnp.zeros_like(base)
-    for f in range(fields):
-        load(f, 0).wait()
+    load(0).wait()
 
     def prefix(f, c, w, v):
         p = jnp.where(w, v, 0.0)
@@ -357,7 +385,7 @@
             rough = rough + fold(base[f, :, lanes(c)])
         pivot[f] = jnp.broadcast_to(across(rough) * (1.0 / (WINDOW * assets)), zero.shape)
 
-    def window_tile(ref, here, first, i, pivots):
+    def window_tile(ref, here, first, i, pivots, which):
         slot = pl.ds(pl.multiple_of(i * TILE, TILE), TILE)
         n = zero
         s = [zero] * fields
@@ -366,7 +394,7 @@
             t, o, u, w = listed(c, first)
             n = n + fold(jnp.where(w, 1.0, 0.0))
             part = share(t, o, u, w)
-            for f in range(fields):
+            for f in which:
                 p = prefix(f, c, w, ref[f, here, lanes(c)])
                 old = ring[f, slot, lanes(c)]
                 ring[f, slot, lanes(c)] = p
@@ -376,13 +404,14 @@
                 s[f] = s[f] + fold(d)
                 q[f] = q[f] + fold(d * d)
         count = across(n)
-        means, columns = moments(count, s, q, pivots, every)
+        means, columns = moments(
+            count, [s[f] for f in which], [q[f] for f in which], [pivots[f] for f in which], which)
         return means, flat(columns + counts_at(count, 2 * width))
 
     def bulk_tile(b, i, pivots):
         r = b * wt + i
         here = pl.ds(pl.multiple_of(r * TILE, TILE), TILE)
-        means, line = window_tile(out, here, t0 + r * TILE, i, pivots)
+        means, line = window_tile(out, here, t0 + r * TILE, i, pivots, every)
         at = pl.ds(r - wt, 1)
         msg_b1[at, :] = msg_b1[at, :] + line
         return means
@@ -411,8 +440,7 @@
     for b in range(1, rows // WINDOW):
         hear(b - 1)
         tell(b)
-        for f in range(fields):
-            load(f, b).wait()
+        load(b).wait()
         bulk_block(b)
     hear(rows // WINDOW - 1)
     exchange_start(0, msg_b1, got_b1)
@@ -425,7 +453,7 @@
     def scaled(center, spread):
         inv = 1.0 / jnp.sqrt(jnp.maximum(spread, 0.0) + 0.1)
         wide = lax.broadcasted_iota(jnp.int32, center.shape, 1)
-        return jnp.where(wide < width, center, pltpu.roll(inv, width, 1))
+        return jnp.where(wide % (2 * width) < width, center, pltpu.roll(inv, width, 1))
 
     def left(v, by):
         return pltpu.roll(v, LANES - by, 1)
@@ -461,34 +489,36 @@
     def summed(got):
         return sum_over(lambda p: got[p], got.shape[1:])
 
-    def apply_tile(ref, r, row, row_in, clipping, keep=True):
+    def columns_of(row_in, row, which, at=0):
+        line = jnp.broadcast_to(row_in[pl.ds(row, 1), :], zero.shape)
+        center = {f: column(line, at + f * TILE) for f in which}
+        inv = {f: column(line, at + width + f * TILE) for f in which}
+        return center, inv
+
+    def clipped_sums(ref, r, row, row_in, which, mark=0.0, at=0):
         here = pl.ds(pl.multiple_of(r * TILE, TILE), TILE)
         first = t0 + r * TILE if ref is out else t0 + rows + r * TILE
-        line = jnp.broadcast_to(row_in[pl.ds(row, 1), :], zero.shape)
-        center = [column(line, f * TILE) for f in range(fields)]
-        inv = [column(line, width + f * TILE) for f in range(fields)]
-        s = [zero] * fields
-        q = [zero] * fields
+        center, inv = columns_of(row_in, row, which)
+        s = {f: zero for f in which}
+        q = {f: zero for f in which}
         for c in range(chunks):
             _, _, _, w = listed(c, first)
-            for f in range(fields):
+            for f in which:
                 y = (ref[f, here, lanes(c)] - center[f]) * inv[f]
-                if clipping:
-                    y = jnp.clip(y, -3.0, 3.0)
+                y = jnp.clip(y, -3.0, 3.0)
+                if ref is out:
+                    ref[f, here, lanes(c)] = jnp.where(w, y, mark)
                 y = jnp.where(w, y, 0.0)
-                if keep:
-                    ref[f, here, lanes(c)] = y
-                if clipping:
-                    s[f] = s[f] + fold(y)
-                    q[f] = q[f] + fold(y * y)
-        return s, q
-
-    def clip_tile(ref, r, row, row_in, msg, msg_row):
-        s, q = apply_tile(ref, r, row, row_in, True, ref is out)
+                s[f] = s[f] + fold(y)
+                q[f] = q[f] + fold(y * y)
         columns = []
-        for f in range(fields):
-            columns.append((f * TILE, across(s[f])))
-            columns.append((width + f * TILE, across(q[f])))
+        for f in which:
+            columns.append((at + f * TILE, across(s[f])))
+            columns.append((at + width + f * TILE, across(q[f])))
+        return columns
+
+    def clip_tile(ref, r, row, row_in, msg, msg_row, which, mark=0.0):
+        columns = clipped_sums(ref, r, row, row_in, which, mark)
         msg[pl.ds(msg_row, 1), :] = flat(columns)
 
     def merge2(got, floor, rows_out):
@@ -497,8 +527,14 @@
         spread = left(sums, width) / floor - center * center
         rows_out[...] = scaled(center, spread)
 
-    def final_tile(r, row, row_in):
-        apply_tile(out, r, row, row_in, False)
+    def final_tile(r, row, row_in, which, at=0):
+        here = pl.ds(pl.multiple_of(r * TILE, TILE), TILE)
+        center, inv = columns_of(row_in, row, which, at)
+        for c in range(chunks):
+            _, _, _, w = listed(c, t0 + r * TILE)
+            for f in which:
+                y = (out[f, here, lanes(c)] - center[f]) * inv[f]
+                out[f, here, lanes(c)] = jnp.where(w, y, 0.0)
 
     def over(n, step, unroll=1):
         def one(i, carry):
@@ -507,9 +543,13 @@
 
         lax.fori_loop(0, n, one, 0, unroll=unroll)
 
-    def arrival(f, r):
-        k = around.index((f, r)) if (f, r) in around else None
-        return direct(f, r) if k is None else relay2(k)
+    def arrival(f, r, h):
+        if (f, r, h) in around:
+            relay2(around.index((f, r, h))).wait_recv()
+        elif h == 0:
+            for i, (tile, cut) in enumerate(straight):
+                if tile == r and cut[0] == f:
+                    direct(i).wait_recv()
 
     def joined(f, c, here, past):
         h = jnp.where(past, halo[f, here, lanes(c)], 0.0)
@@ -525,56 +565,65 @@
         _, _, _, past = listed(c, t0 + r * TILE - WINDOW)
         return past & (t >= WINDOW)
 
-    def halo_part(r, msg, row, extra):
+    def halo_part(r, msg, row, counted_too, which):
         here = tile_rows(r)
-        s = [zero] * fields
-        q = [zero] * fields
-        pivots = [ahead[f][:, :1] for f in every]
+        s = {f: zero for f in which}
+        q = {f: zero for f in which}
+        pivots = {f: ahead[f][:, :1] for f in which}
         for c in range(chunks):
             t, o, u, w = listed(c, t0 + r * TILE)
             past = before_mask(c, t, r)
             part = share(t, o, u, w)
-            for f in every:
+            for f in which:
                 rolled = joined(f, c, here, past) * part
                 out[f, here, lanes(c)] = rolled
                 d = jnp.where(w, rolled - pivots[f], 0.0)
                 s[f] = s[f] + fold(d)
                 q[f] = q[f] + fold(d * d)
         count = local_count[r][:, :1]
-        means, columns = moments(count, s, q, pivots, every)
-        for f in every:
-            ahead[f] = jnp.broadcast_to(means[f], zero.shape)
-        if extra:
+        means, columns = moments(
+            count,
+            [s[f] for f in which],
+            [q[f] for f in which],
+            [pivots[f] for f in which],
+            which,
+        )
+        for f, mean in zip(which, means):
+            ahead[f] = jnp.broadcast_to(mean, zero.shape)
+        if counted_too:
             columns = columns + counts_at(count, 2 * width)
-        msg[pl.ds(row, 1), :] = flat(columns)
-
-    def group_tile(r):
+        at = pl.ds(row, 1)
+        msg[at, :] = msg[at, :] + flat(columns)
+
+    def group_tile(r, which):
         @pl.when(has_prev)
         def _():
-            for f in every:
-                arrival(f, r).wait_recv()
-
-        halo_part(r, msg_g1, wt - 1 - r, False)
+            for f in which:
+                arrival(f, r, 0)
+
+        halo_part(r, msg_g1, wt - 1 - r, False, which)
 
     def finish(r, which):
         here = tile_rows(r)
-        lines = [jnp.broadcast_to(told[i, pl.ds(r, 1), :], zero.shape) for i in range(2)]
-        center = [[column(line, f * TILE) for f in which] for line in lines]
-        inv = [[column(line, width + f * TILE) for f in which] for line in lines]
-        for f in which:
-            arrival(f, r).wait_recv()
-        for c in range(chunks):
-            t, o, u, w = listed(c, t0 + r * TILE)
-            past = before_mask(c, t, r)
-            part = share(t, o, u, w)
-            for i, f in enumerate(which):
-                rolled = joined(f, c, here, past) * part
-                y = jnp.clip((rolled - center[0][i]) * inv[0][i], -3.0, 3.0)
-                y = (y - center[1][i]) * inv[1][i]
-                out[f, here, lanes(c)] = jnp.where(w, y, 0.0)
+        first = columns_of(told.at[0], r, which)
+        then = columns_of(told.at[1], r, which)
+        per = chunks // HALVES
+        for h in range(HALVES):
+            for f in which:
+                arrival(f, r, h)
+            for c in range(h * per, (h + 1) * per):
+                t, o, u, w = listed(c, t0 + r * TILE)
+                past = before_mask(c, t, r)
+                part = share(t, o, u, w)
+                for f in which:
+                    y = joined(f, c, here, past) * part
+                    y = jnp.clip((y - first[0][f]) * first[1][f], -3.0, 3.0)
+                    y = (y - then[0][f]) * then[1][f]
+                    out[f, here, lanes(c)] = jnp.where(w, y, 0.0)
 
     suffix[...] = jnp.zeros_like(suffix)
     msg_e1[...] = jnp.zeros_like(msg_e1)
+    msg_g1[...] = jnp.zeros_like(msg_g1)
     msg_e2[...] = jnp.zeros_like(msg_e2)
 
 
@@ -583,13 +632,13 @@
         def _():
             pass2(ks)
 
-    group_tile(7)
-    group_tile(6)
+    group_tile(7, every)
+    group_tile(6, every)
 
     @pl.when(x == 0)
     def _():
-        for r in range(EARLY - 1, -1, -1):
-            halo_part(r, msg_e1, EARLY + r, True)
+        for r in range(tops - 1, -1, -1):
+            halo_part(r, msg_e1, tops + r, True, early(r))
 
     exchange_all(0, got_b1).wait_recv()
 
@@ -603,29 +652,39 @@
     floor_b[...] = jnp.maximum(left(sums, 2 * width), 1.0)
     floor_h[...] = jnp.maximum(left(sums[:wt, :], 3 * width), 1.0)
     merge(got_b1, lambda p: count_b[p], floor_b[...], left(sums, width), row_b1)
-    group_tile(5)
+    group_tile(5, every)
 
     @pl.when(has_next)
     def _():
         total[...] = base[...]
         base[...] = jnp.zeros_like(base)
-        extension.wait_recv()
-
-        def one(r, carry):
+        for copy in extensions:
+            copy.wait_recv()
+
+        def one(r, which):
             here = pl.ds(pl.multiple_of(r * TILE, TILE), TILE)
             pivots = [pivot[f][:, :1] for f in every]
-            means, line = window_tile(ext, here, t0 + rows + r * TILE, r, pivots)
-            for f in every:
-                pivot[f] = jnp.broadcast_to(means[f], zero.shape)
+            means, line = window_tile(ext, here, t0 + rows + r * TILE, r, pivots, which)
+            for f, mean in zip(which, means):
+                pivot[f] = jnp.broadcast_to(mean, zero.shape)
             msg_e1[pl.ds(r, 1), :] = line
-            return carry
-
-        lax.fori_loop(0, EARLY, one, 0)
+
+        over(EARLY, lambda r: one(r, every))
+        if EXTRA:
+            one(EARLY, extra)
 
     exchange_start(2, msg_e1, got_e1)
-    over(bulk, lambda i: clip_tile(out, i + wt, i, row_b1, msg_b2, i), 2)
+    pairs = bulk // 2
+
+    def clip_pair(j):
+        columns = clipped_sums(out, j + wt, j, row_b1, every)
+        i = j + pairs
+        columns += clipped_sums(out, i + wt, i, row_b1, every, at=2 * width)
+        msg_b2[pl.ds(j, 1), :] = flat(columns)
+
+    over(pairs, clip_pair)
     exchange_start(1, msg_b2, got_b2)
-    some = range(4)
+    some = range(6)
 
     @pl.when(x < blocks_t - 2)
     def _():
@@ -635,6 +694,7 @@
     def _():
         pass2(some)
 
+    group_tile(4, every)
     exchange_all(2, got_e1).wait_recv()
 
     def split_e(p):
@@ -648,18 +708,17 @@
 
     @pl.when(has_next)
     def _():
-        over(EARLY, lambda r: clip_tile(ext, r, r, first_params, msg_e2, r))
+        over(EARLY, lambda r: clip_tile(ext, r, r, first_params, msg_e2, r, every))
+        for r in range(EARLY, tops):
+            clip_tile(ext, r, r, first_params, msg_e2, r, extra)
 
     @pl.when(x == 0)
     def _():
-        over(
-            EARLY,
-            lambda r: clip_tile(out, r, EARLY + r, first_params, msg_e2, EARLY + r),
-        )
+        for r in range(tops):
+            clip_tile(out, r, tops + r, first_params, msg_e2, tops + r, early(r))
 
     exchange_start(3, msg_e2, got_e2)
-    group_tile(4)
-    rest = range(4, len(around))
+    rest = range(6, len(around))
 
     @pl.when(x < blocks_t - 2)
     def _():
@@ -669,34 +728,47 @@
     def _():
         pass2(rest)
 
-    second([0])
-    group_tile(3)
+    group_tile(3, kept[:-1])
+    group_tile(3, kept[-1:])
     exchange_start(4, msg_g1, got_g1)
-    second([1])
+    second([0,1])
+    second([2,3])
     exchange_all(3, got_e2).wait_recv()
     merge2(got_e2, floor_e, second_params)
 
     @pl.when(has_next)
     def _():
         telling.start()
+        direct(len(straight) - 1).start()
 
 
     @pl.when(x == 0)
     def _():
-        over(EARLY, lambda r: final_tile(r, EARLY + r, second_params))
-
-    second([2,3])
+        for r in range(tops):
+            final_tile(r, tops + r, second_params, early(r))
+
+    second([4,5])
     front = wt - EARLY
     exchange_all(4, got_g1).wait_recv()
-    second([4])
+    second([6,7])
     m2 = left(summed(got_g1), width)
     merge(got_g1, lambda p: count_h[p, :front, :], floor_h[:front, :], m2, row_g1)
-    over(front, lambda i: clip_tile(out, wt - 1 - i, i, row_g1, msg_g2, i), front)
+    for r in range(wt - 1, EARLY - 1, -1):
+        i = wt - 1 - r
+        clip_tile(out, r, i, row_g1, msg_g2, i, grouped(r), MARK)
     exchange_start(5, msg_g2, got_g2)
-    second([5])
+    second([8,9])
     exchange_all(1, got_b2).wait_recv()
-    merge2(got_b2, floor_b[...], row_b2)
-    over(bulk, lambda i: final_tile(i + wt, i, row_b2), 2)
+    low, high = floor_b[pl.ds(0, pairs), :], floor_b[pl.ds(pairs, pairs), :]
+    wide = lax.broadcasted_iota(jnp.int32, low.shape, 1)
+    both = jnp.where(wide < 2 * width, low, pltpu.roll(high, 2 * width, 1))
+    merge2(got_b2, both, row_b2)
+
+    def final_pair(j):
+        final_tile(j + wt, j, row_b2, every)
+        final_tile(j + pairs + wt, j, row_b2, every, 2 * width)
+
+    over(pairs, final_pair)
 
 
     @pl.when(has_prev)
@@ -706,29 +778,29 @@
 
     @pl.when(has_prev)
     def _():
+        for r in range(EARLY, tops):
+            finish(r, extra)
         for r in range(EARLY - 1, -1, -1):
-            finish(r, fore)
-        for r in range(EARLY - 1, -1, -1):
-            finish(r, rear)
+            finish(r, [f for f in every if (f, r) not in BACK])
+            finish(r, [f for f in every if (f, r) in BACK])
 
     exchange_all(5, got_g2).wait_recv()
-    merge2(got_g2, floor_h[:front, :], row_g2)
-    over(front, lambda i: final_tile(wt - 1 - i, i, row_g2), front)
-
+    merge2(got_g2, floor_h[:front, :], out.at[0, pl.ds(rows, front), pl.ds(0, LANES)])
     for g, got in enumerate((got_b1, got_b2, got_e1, got_e2, got_g1, got_g2)):
         exchange_all(g, got).wait_send()
 
     @pl.when(has_prev)
     def _():
-        extension.wait_send()
+        for copy in extensions:
+            copy.wait_send()
 
     @pl.when(has_next)
     def _():
         telling.wait_send()
         for k in range(len(around)):
             back(k).wait_send()
-        for f, r in straight:
-            direct(f, r).wait_send()
+        for i in range(len(straight)):
+            direct(i).wait_send()
 
     @pl.when(hops1)
     def _():
@@ -739,6 +811,54 @@
     def _():
         for k in range(len(around)):
             relay2(k).wait_send()
+
+
+def writer(x_ref, o_ref, tile_ref, sem, sem_tile):
+    fields, rows, assets = o_ref.shape
+    wt = WINDOW // TILE
+    step = (rows - WINDOW) // 2
+    spans = []
+    for f in range(fields):
+        tops = EARLY + (1 if f >= fields - EXTRA else 0)
+        spans.append((f, 0, tops * TILE))
+        spans.extend((f, WINDOW + i * step, step) for i in range(2))
+    copies = [
+        pltpu.make_async_copy(
+            x_ref.at[f, pl.ds(at, size), :], o_ref.at[f, pl.ds(at, size), :], sem.at[i]
+        )
+        for i, (f, at, size) in enumerate(spans)
+    ]
+    for copy in copies:
+        copy.start()
+    sub = lax.broadcasted_iota(jnp.int32, (TILE, LANES), 0)
+    lane = lax.broadcasted_iota(jnp.int32, (TILE, LANES), 1)
+    width = fields * TILE
+    for i in range(wt - EARLY):
+        r = wt - 1 - i
+        many = fields if r > EARLY else fields - EXTRA
+        here, there = pl.ds(r * TILE, TILE), pl.ds(i * TILE, TILE)
+        line = jnp.broadcast_to(x_ref[0, pl.ds(rows + i, 1), :LANES], (TILE, LANES))
+
+        def column(at):
+            kept = jnp.where(lane == sub + at, line, 0.0)
+            return jnp.sum(kept, axis=1, keepdims=True)
+
+        for f in range(many):
+            center, inv = column(f * TILE), column(width + f * TILE)
+            for c in range(assets // CHUNK):
+                part = pl.ds(c * CHUNK, CHUNK)
+                y = x_ref[f, here, part]
+                z = jnp.where(y > 3.5, 0.0, (y - center) * inv)
+                tile_ref[f, there, part] = z
+        copy = pltpu.make_async_copy(
+            tile_ref.at[pl.ds(0, many), there, :],
+            o_ref.at[pl.ds(0, many), here, :],
+            sem_tile.at[i],
+        )
+        copy.start()
+        copies.append(copy)
+    for copy in copies:
+        copy.wait()
 
 
 def per_device(blocks_t, peers, values, listed_from, listed_until):
@@ -749,8 +869,9 @@
     f32 = jnp.float32
     vmem = pltpu.VMEM
     dma = pltpu.SemaphoreType.DMA
-    around = EARLY * LATE
-    groups = (bulk, bulk, 2 * EARLY, 2 * EARLY, wt - EARLY, wt - EARLY)
+    around = len(BACK) * HALVES
+    tops = EARLY + (1 if EXTRA else 0)
+    groups = (bulk, bulk // 2, 2 * tops, 2 * tops, wt - EARLY, wt - EARLY)
     scratch = [
         vmem((1, assets), jnp.int32),
         vmem((1, assets), jnp.int32),
@@ -758,11 +879,11 @@
         pltpu.SemaphoreType.REGULAR((4,)),
         vmem((wt, TILE, LANES), f32),
         vmem((fields, WINDOW, assets), f32),
-        vmem((around * TILE, assets), f32),
-        vmem((around * TILE, assets), f32),
-        vmem((fields, EARLY * TILE, assets), f32),
-        vmem((2, 2 * EARLY, LANES), f32),
-        vmem((2, 2 * EARLY, LANES), f32),
+        vmem((around * TILE, assets // HALVES), f32),
+        vmem((around * TILE, assets // HALVES), f32),
+        vmem((fields, tops * TILE, assets), f32),
+        vmem((2, 2 * tops, LANES), f32),
+        vmem((2, 2 * tops, LANES), f32),
         vmem((fields, WINDOW, assets), f32),
         vmem((fields, TILE, assets), f32),
         vmem((fields, TILE, assets), f32),
@@ -771,27 +892,28 @@
         vmem((fields, TILE, LANES), f32),
         *[vmem((n, LANES), f32) for n in groups],
         *[vmem((peers, n, LANES), f32) for n in groups],
-        *[vmem((peers, n, LANES), f32) for n in (bulk, 2 * EARLY, wt)],
+        *[vmem((peers, n, LANES), f32) for n in (bulk, 2 * tops, wt)],
         *[vmem((n, LANES), f32) for n in (bulk, wt)],
-        *[vmem((n, LANES), f32) for n in (bulk, bulk, wt - EARLY, wt - EARLY)],
-        dma((fields, rows // WINDOW)),
+        *[vmem((n, LANES), f32) for n in (bulk, bulk // 2, wt - EARLY)],
+        dma((rows // WINDOW,)),
+        dma,
+        dma((2,)),
+        dma((2,)),
         dma,
         dma,
         dma,
         dma,
         dma,
-        dma,
-        dma,
-        dma,
-        dma((fields, wt)),
+        dma((wt + 2,)),
+        dma((around,)),
         dma((around,)),
         dma((around,)),
         dma((6,)),
         dma((6,)),
     ]
-    return pl.pallas_call(
+    clipped = pl.pallas_call(
         functools.partial(kernel, (blocks_t, peers)),
-        out_shape=pltpu.VMEM(values.shape, values.dtype),
+        out_shape=pltpu.VMEM((fields, rows + TILE, assets), values.dtype),
         in_specs=[
             pl.BlockSpec(memory_space=pltpu.HBM),
             pl.BlockSpec(memory_space=pltpu.HBM),
@@ -805,6 +927,18 @@
             vmem_limit_bytes=48 * 1024 * 1024,
         ),
     )(values, listed_from[None, :], listed_until[None, :])
+    return pl.pallas_call(
+        writer,
+        out_shape=jax.ShapeDtypeStruct(values.shape, values.dtype),
+        in_specs=[pl.BlockSpec(memory_space=pltpu.VMEM)],
+        out_specs=pl.BlockSpec(memory_space=pltpu.HBM),
+        scratch_shapes=[
+            vmem((fields, WINDOW - EARLY * TILE, assets), f32),
+            dma((3 * fields,)),
+            dma((wt - EARLY,)),
+        ],
+        compiler_params=pltpu.CompilerParams(vmem_limit_bytes=8 * 1024 * 1024),
+    )(pltpu.with_memory_space_constraint(clipped, pltpu.VMEM))
 
 
 def solution(mesh):

time: 51.6 us -> 50.7 us (0.983)
  local copies, waits for them, and re-layouts: 3.4 us -> 0 us
  Pallas kernels: 48.1 us -> 50.6 us
    pallas_call x0 -> x1, Pallas kernels: none -> 3.42 us  [per_device(): pl.pallas_call(writer, out_shape=jax.ShapeDtypeStruct(values.shape, value...]
    unnamed x1 -> x0, local copies, waits for them, and re-layouts: 3.4 us -> none
    pallas_call x1, Pallas kernels: 48.1 us -> 47.1 us  [per_device(): pl.pallas_call(functools.partial(kernel, (blocks_t, peers)), out_shape=pl...]
where the time goes in v4:
time: 50.7 us; the launch traced here: 50.6 us
  Pallas kernels  50.6 us (100%)
    pallas_call x1, Pallas kernels, per_device(): pl.pallas_call(functools.partial(kernel, (blocks_t, peers)), out_shape=pl...  47.1 us
    pallas_call x1, Pallas kernels, per_device(): pl.pallas_call(writer, out_shape=jax.ShapeDtypeStruct(values.shape, value...  3.42 us

profile of v4, /device:TPU:1, one launch (start us, length us, event | category | flops | bytes accessed | tf_op | source)
XLA Modules:
  0.0 50.6 jit_solution(6957151186025153889)
XLA Ops:
  0.0 47.1 %shard_map.37.x_ref = f32[4,264,2048]{2,1,0:T(8,128)S(1)} custom-call(f32[4,256,2048]{2,1,0:T(8,128)} %vals.1, s32[1,2048]{1,0:T(1,128)} %bitcast.2, s32[1,2048]{1,0:T(1,128)} %bitcast.3), custom_call_target="tpu_custom_call" | custom-call | tf_op jit(solution)/shard_map/pallas_call | solution.py:914
  47.2 3.4 %shard_map.38 = f32[4,256,2048]{2,1,0:T(8,128)} custom-call(f32[4,264,2048]{2,1,0:T(8,128)S(1)} %shard_map.37.x_ref), custom_call_target="tpu_custom_call" | custom-call | tf_op jit(solution)/shard_map/pallas_call | solution.py:930

commit v5 on v4

--- a/solution.py
+++ b/solution.py
@@ -13,6 +13,7 @@
 EXTRA = 1
 HALVES = 2
 MARK = 4.0
+DEEP = 3
 TILE = 8
 LANES = 128
 CHUNK = 512
@@ -139,6 +140,11 @@
     def tile_rows(r):
         return pl.ds(r * TILE, TILE)
 
+    def needed(at, r):
+        skip = 1 if r == 0 else 0
+        return pl.ds(at + skip, TILE - skip)
+
+
     every = list(range(fields))
     kept, extra = every[: fields - EXTRA], every[fields - EXTRA :]
     tops = EARLY + (1 if EXTRA else 0)
@@ -170,8 +176,8 @@
         r, cut = straight[i]
         which = pl.ds(cut[0], len(cut))
         return pltpu.make_async_remote_copy(
-            src_ref=vals.at[which, pl.ds(tail + r * TILE, TILE), :],
-            dst_ref=halo.at[which, tile_rows(r), :],
+            src_ref=vals.at[which, needed(tail + r * TILE, r), :],
+            dst_ref=halo.at[which, needed(r * TILE, r), :],
             send_sem=direct_send,
             recv_sem=halo_recv.at[i],
             device_id={"tm": nxt},
@@ -181,8 +187,8 @@
     def back(k):
         f, r, h = around[k]
         return pltpu.make_async_remote_copy(
-            src_ref=vals.at[f, pl.ds(tail + r * TILE, TILE), half(h)],
-            dst_ref=hop1.at[tile_rows(k), :],
+            src_ref=vals.at[f, needed(tail + r * TILE, r), half(h)],
+            dst_ref=hop1.at[needed(k * TILE, r), :],
             send_sem=back_send,
             recv_sem=hop1_recv.at[k],
             device_id={"tm": prv},
@@ -190,9 +196,10 @@
         )
 
     def relay1(k):
+        part = needed(k * TILE, around[k][1])
         return pltpu.make_async_remote_copy(
-            src_ref=hop1.at[tile_rows(k), :],
-            dst_ref=hop2.at[tile_rows(k), :],
+            src_ref=hop1.at[part, :],
+            dst_ref=hop2.at[part, :],
             send_sem=relay1_send,
             recv_sem=hop2_recv.at[k],
             device_id={"tm": prv},
@@ -202,8 +209,8 @@
     def relay2(k):
         f, r, h = around[k]
         return pltpu.make_async_remote_copy(
-            src_ref=hop2.at[tile_rows(k), :],
-            dst_ref=halo.at[f, tile_rows(r), half(h)],
+            src_ref=hop2.at[needed(k * TILE, r), :],
+            dst_ref=halo.at[f, needed(r * TILE, r), half(h)],
             send_sem=relay2_send,
             recv_sem=back_recv.at[k],
             device_id={"tm": prv},
@@ -495,10 +502,10 @@
         inv = {f: column(line, at + width + f * TILE) for f in which}
         return center, inv
 
-    def clipped_sums(ref, r, row, row_in, which, mark=0.0, at=0):
+    def clipped_sums(ref, r, row, row_in, which, mark=0.0, at=0, read=0):
         here = pl.ds(pl.multiple_of(r * TILE, TILE), TILE)
         first = t0 + r * TILE if ref is out else t0 + rows + r * TILE
-        center, inv = columns_of(row_in, row, which)
+        center, inv = columns_of(row_in, row, which, read)
         s = {f: zero for f in which}
         q = {f: zero for f in which}
         for c in range(chunks):
@@ -592,8 +599,9 @@
             ahead[f] = jnp.broadcast_to(mean, zero.shape)
         if counted_too:
             columns = columns + counts_at(count, 2 * width)
-        at = pl.ds(row, 1)
-        msg[at, :] = msg[at, :] + flat(columns)
+        at = pl.ds(row % DEEP if msg is msg_g1 else row, 1)
+        shift = 2 * width * (row // DEEP) if msg is msg_g1 else 0
+        msg[at, :] = msg[at, :] + flat([(n + shift, v) for n, v in columns])
 
     def group_tile(r, which):
         @pl.when(has_prev)
@@ -642,15 +650,19 @@
 
     exchange_all(0, got_b1).wait_recv()
 
+    def doubled(v):
+        high = pltpu.roll(pltpu.roll(v, wt - DEEP, 0), 2 * width, 1)
+        return jnp.where(lane < 2 * width, v, high)
+
     def split(p):
         v = got_b1[p]
         count_b[p] = left(v, 2 * width)
-        count_h[p] = left(v[:wt, :], 3 * width)
+        count_h[p] = doubled(left(v[:wt, :], 3 * width))
 
     over(peers, split, 8)
     sums = summed(got_b1)
     floor_b[...] = jnp.maximum(left(sums, 2 * width), 1.0)
-    floor_h[...] = jnp.maximum(left(sums[:wt, :], 3 * width), 1.0)
+    floor_h[...] = jnp.maximum(doubled(left(sums[:wt, :], 3 * width)), 1.0)
     merge(got_b1, lambda p: count_b[p], floor_b[...], left(sums, width), row_b1)
     group_tile(5, every)
 
@@ -703,19 +715,22 @@
     over(peers, split_e, peers)
     sums = summed(got_e1)
     floor_e = jnp.maximum(left(sums, 2 * width), 1.0)
-    first_params, second_params = params.at[0], params.at[1]
+    first_params, second_params = params.at[0], params.at[1, pl.ds(0, tops)]
     merge(got_e1, lambda p: count_e[p], floor_e, left(sums, width), first_params)
 
     @pl.when(has_next)
     def _():
-        over(EARLY, lambda r: clip_tile(ext, r, r, first_params, msg_e2, r, every))
-        for r in range(EARLY, tops):
-            clip_tile(ext, r, r, first_params, msg_e2, r, extra)
+        for r in range(tops):
+            clip_tile(ext, r, r, first_params, msg_e2, r, early(r))
 
     @pl.when(x == 0)
     def _():
         for r in range(tops):
-            clip_tile(out, r, tops + r, first_params, msg_e2, tops + r, early(r))
+            columns = clipped_sums(
+                out, r, tops + r, first_params, early(r), at=2 * width
+            )
+            at = pl.ds(r, 1)
+            msg_e2[at, :] = msg_e2[at, :] + flat(columns)
 
     exchange_start(3, msg_e2, got_e2)
     rest = range(6, len(around))
@@ -734,6 +749,9 @@
     second([0,1])
     second([2,3])
     exchange_all(3, got_e2).wait_recv()
+    upper = pltpu.roll(pltpu.roll(floor_e, tops, 0), 2 * width, 1)
+    wide = lax.broadcasted_iota(jnp.int32, floor_e.shape, 1)
+    floor_e = jnp.where(wide < 2 * width, floor_e, upper)[:tops, :]
     merge2(got_e2, floor_e, second_params)
 
     @pl.when(has_next)
@@ -745,17 +763,22 @@
     @pl.when(x == 0)
     def _():
         for r in range(tops):
-            final_tile(r, tops + r, second_params, early(r))
+            final_tile(r, r, second_params, early(r), 2 * width)
 
     second([4,5])
-    front = wt - EARLY
     exchange_all(4, got_g1).wait_recv()
     second([6,7])
     m2 = left(summed(got_g1), width)
-    merge(got_g1, lambda p: count_h[p, :front, :], floor_h[:front, :], m2, row_g1)
+    merge(got_g1, lambda p: count_h[p, :DEEP, :], floor_h[:DEEP, :], m2, row_g1)
+    packed = [[] for _ in range(DEEP)]
     for r in range(wt - 1, EARLY - 1, -1):
         i = wt - 1 - r
-        clip_tile(out, r, i, row_g1, msg_g2, i, grouped(r), MARK)
+        at = 2 * width * (i // DEEP)
+        packed[i % DEEP] += clipped_sums(
+            out, r, i % DEEP, row_g1, grouped(r), MARK, at, at
+        )
+    for i in range(DEEP):
+        msg_g2[pl.ds(i, 1), :] = flat(packed[i])
     exchange_start(5, msg_g2, got_g2)
     second([8,9])
     exchange_all(1, got_b2).wait_recv()
@@ -785,7 +808,7 @@
             finish(r, [f for f in every if (f, r) in BACK])
 
     exchange_all(5, got_g2).wait_recv()
-    merge2(got_g2, floor_h[:front, :], out.at[0, pl.ds(rows, front), pl.ds(0, LANES)])
+    merge2(got_g2, floor_h[:DEEP, :], out.at[0, pl.ds(rows, DEEP), pl.ds(0, LANES)])
     for g, got in enumerate((got_b1, got_b2, got_e1, got_e2, got_g1, got_g2)):
         exchange_all(g, got).wait_send()
 
@@ -837,14 +860,17 @@
         r = wt - 1 - i
         many = fields if r > EARLY else fields - EXTRA
         here, there = pl.ds(r * TILE, TILE), pl.ds(i * TILE, TILE)
-        line = jnp.broadcast_to(x_ref[0, pl.ds(rows + i, 1), :LANES], (TILE, LANES))
+        row = x_ref[0, pl.ds(rows + i % DEEP, 1), :LANES]
+        line = jnp.broadcast_to(row, (TILE, LANES))
+        shift = 2 * width * (i // DEEP)
 
         def column(at):
             kept = jnp.where(lane == sub + at, line, 0.0)
             return jnp.sum(kept, axis=1, keepdims=True)
 
         for f in range(many):
-            center, inv = column(f * TILE), column(width + f * TILE)
+            center = column(shift + f * TILE)
+            inv = column(shift + width + f * TILE)
             for c in range(assets // CHUNK):
                 part = pl.ds(c * CHUNK, CHUNK)
                 y = x_ref[f, here, part]
@@ -871,7 +897,7 @@
     dma = pltpu.SemaphoreType.DMA
     around = len(BACK) * HALVES
     tops = EARLY + (1 if EXTRA else 0)
-    groups = (bulk, bulk // 2, 2 * tops, 2 * tops, wt - EARLY, wt - EARLY)
+    groups = (bulk, bulk // 2, 2 * tops, tops, DEEP, DEEP)
     scratch = [
         vmem((1, assets), jnp.int32),
         vmem((1, assets), jnp.int32),
@@ -894,7 +920,7 @@
         *[vmem((peers, n, LANES), f32) for n in groups],
         *[vmem((peers, n, LANES), f32) for n in (bulk, 2 * tops, wt)],
         *[vmem((n, LANES), f32) for n in (bulk, wt)],
-        *[vmem((n, LANES), f32) for n in (bulk, bulk // 2, wt - EARLY)],
+        *[vmem((n, LANES), f32) for n in (bulk, bulk // 2, DEEP)],
         dma((rows // WINDOW,)),
         dma,
         dma((2,)),

time: 50.7 us -> 49.9 us (0.984)
  Pallas kernels: 50.6 us -> 49.8 us
    pallas_call x1, Pallas kernels: 47.1 us -> 46.4 us  [per_device(): pl.pallas_call(functools.partial(kernel, (blocks_t, peers)), out_shape=pl...]
where the time goes in v5:
time: 49.9 us; the launch traced here: 49.8 us
  Pallas kernels  49.8 us (100%)
    pallas_call x1, Pallas kernels, per_device(): pl.pallas_call(functools.partial(kernel, (blocks_t, peers)), out_shape=pl...  46.4 us
    pallas_call x1, Pallas kernels, per_device(): pl.pallas_call(writer, out_shape=jax.ShapeDtypeStruct(values.shape, value...  3.42 us

profile of v5, /device:TPU:1, one launch (start us, length us, event | category | flops | bytes accessed | tf_op | source)
XLA Modules:
  0.0 49.8 jit_solution(15477226767785514401)
XLA Ops:
  0.0 46.4 %shard_map.37.x_ref = f32[4,264,2048]{2,1,0:T(8,128)S(1)} custom-call(f32[4,256,2048]{2,1,0:T(8,128)} %vals.1, s32[1,2048]{1,0:T(1,128)} %bitcast.2, s32[1,2048]{1,0:T(1,128)} %bitcast.3), custom_call_target="tpu_custom_call" | custom-call | tf_op jit(solution)/shard_map/pallas_call | solution.py:940
  46.4 3.4 %shard_map.38 = f32[4,256,2048]{2,1,0:T(8,128)} custom-call(f32[4,264,2048]{2,1,0:T(8,128)S(1)} %shard_map.37.x_ref), custom_call_target="tpu_custom_call" | custom-call | tf_op jit(solution)/shard_map/pallas_call | solution.py:956

commit v6 on v5

--- a/solution.py
+++ b/solution.py
@@ -681,7 +681,7 @@
                 pivot[f] = jnp.broadcast_to(mean, zero.shape)
             msg_e1[pl.ds(r, 1), :] = line
 
-        over(EARLY, lambda r: one(r, every))
+        over(EARLY, lambda r: one(r, every), EARLY)
         if EXTRA:
             one(EARLY, extra)
 

time: 49.9 us -> 49.7 us (level)
  no operation moved by 1% of the time
where the time goes in v6:
time: 49.7 us; the launch traced here: 49.6 us
  Pallas kernels  49.6 us (100%)
    pallas_call x1, Pallas kernels, per_device(): pl.pallas_call(functools.partial(kernel, (blocks_t, peers)), out_shape=pl...  46.2 us
    pallas_call x1, Pallas kernels, per_device(): pl.pallas_call(writer, out_shape=jax.ShapeDtypeStruct(values.shape, value...  3.42 us

profile of v6, /device:TPU:1, one launch (start us, length us, event | category | flops | bytes accessed | tf_op | source)
XLA Modules:
  0.0 49.6 jit_solution(899832189286546255)
XLA Ops:
  0.0 46.2 %shard_map.37.x_ref = f32[4,264,2048]{2,1,0:T(8,128)S(1)} custom-call(f32[4,256,2048]{2,1,0:T(8,128)} %vals.1, s32[1,2048]{1,0:T(1,128)} %bitcast.2, s32[1,2048]{1,0:T(1,128)} %bitcast.3), custom_call_target="tpu_custom_call" | custom-call | tf_op jit(solution)/shard_map/pallas_call | solution.py:940
  46.2 3.4 %shard_map.38 = f32[4,256,2048]{2,1,0:T(8,128)} custom-call(f32[4,264,2048]{2,1,0:T(8,128)S(1)} %shard_map.37.x_ref), custom_call_target="tpu_custom_call" | custom-call | tf_op jit(solution)/shard_map/pallas_call | solution.py:956

commit v7 on v6

--- a/solution.py
+++ b/solution.py
@@ -839,12 +839,12 @@
 def writer(x_ref, o_ref, tile_ref, sem, sem_tile):
     fields, rows, assets = o_ref.shape
     wt = WINDOW // TILE
-    step = (rows - WINDOW) // 2
+    step = (rows - WINDOW) // 4
     spans = []
     for f in range(fields):
         tops = EARLY + (1 if f >= fields - EXTRA else 0)
         spans.append((f, 0, tops * TILE))
-        spans.extend((f, WINDOW + i * step, step) for i in range(2))
+        spans.extend((f, WINDOW + i * step, step) for i in range(4))
     copies = [
         pltpu.make_async_copy(
             x_ref.at[f, pl.ds(at, size), :], o_ref.at[f, pl.ds(at, size), :], sem.at[i]
@@ -960,7 +960,7 @@
         out_specs=pl.BlockSpec(memory_space=pltpu.HBM),
         scratch_shapes=[
             vmem((fields, WINDOW - EARLY * TILE, assets), f32),
-            dma((3 * fields,)),
+            dma((5 * fields,)),
             dma((wt - EARLY,)),
         ],
         compiler_params=pltpu.CompilerParams(vmem_limit_bytes=8 * 1024 * 1024),

time: 49.7 us -> 49.8 us (level)
  no operation moved by 1% of the time
where the time goes in v7:
time: 49.8 us; the launch traced here: 49.7 us
  Pallas kernels  49.7 us (100%)
    pallas_call x1, Pallas kernels, per_device(): pl.pallas_call(functools.partial(kernel, (blocks_t, peers)), out_shape=pl...  46.2 us
    pallas_call x1, Pallas kernels, per_device(): pl.pallas_call(writer, out_shape=jax.ShapeDtypeStruct(values.shape, value...  3.48 us

profile of v7, /device:TPU:1, one launch (start us, length us, event | category | flops | bytes accessed | tf_op | source)
XLA Modules:
  0.0 49.7 jit_solution(143438866199312520)
XLA Ops:
  0.0 46.2 %shard_map.37.x_ref = f32[4,264,2048]{2,1,0:T(8,128)S(1)} custom-call(f32[4,256,2048]{2,1,0:T(8,128)} %vals.1, s32[1,2048]{1,0:T(1,128)} %bitcast.2, s32[1,2048]{1,0:T(1,128)} %bitcast.3), custom_call_target="tpu_custom_call" | custom-call | tf_op jit(solution)/shard_map/pallas_call | solution.py:940
  46.2 3.5 %shard_map.38 = f32[4,256,2048]{2,1,0:T(8,128)} custom-call(f32[4,264,2048]{2,1,0:T(8,128)S(1)} %shard_map.37.x_ref), custom_call_target="tpu_custom_call" | custom-call | tf_op jit(solution)/shard_map/pallas_call | solution.py:956
